TPU v7x, 32 devices: a whole 2x2x4 slice. The times are simulated.
32 devices in a mesh: gx: 4 (over x, core), gy: 4 (over z), gz: 2 (over y).
Axes of the slice: x: 2, y: 2, z: 4, core: 2. Of those that a mesh axis runs over, the one named last changes fastest.
Arguments:
- velocity: float32 [3, 32, 128, 512], P(None, 'gz', 'gy', 'gx'), may hold values from -14 to 14, as said below
- geometry: bfloat16 [6, 32, 128, 512], P(None, 'gz', 'gy', 'gx'), may hold values from -0.015 to 0.041, as said below
- mass_weights: bfloat16 [32, 128, 512], P('gz', 'gy', 'gx'), may hold values from 0.0099487305 to 0.099609375
Outputs:
- residual: float32 [3, 32, 128, 512], P(None, 'gz', 'gy', 'gx')
- kinetic: float32 [], replicated
- enstrophy: float32 [], replicated
Inputs may be any that keep to these rules, and one draw needn't show every extreme that they name: `velocity`: coincident points of neighbouring elements hold equal values, and points on the outer boundary of the grid hold zero. `geometry`: at every point the matrix [[g0, g3, g4], [g3, g1, g5], [g4, g5, g2]] is positive definite.
All inputs are finite; a program needn't handle non-finite values.
Results may differ from a plain program's by a relative error of at most 0.0003.
Values sent between devices are 32-bit elements; how exact they have to be, the bound alone decides.
No kernel may reach another device: no remote copies, remote signals or barrier semaphores. Data moves between devices by JAX's collectives and lax.ppermute only.
A program may use at most 128 MiB of HBM per device.

v0:
```python
import functools

import jax
import jax.numpy as jnp
import numpy as np
from jax import lax
from jax.experimental import pallas as pl
from jax.experimental.pallas import tpu as pltpu
from jax.sharding import PartitionSpec as P


ORDER = 7
PTS = ORDER + 1
F32 = jnp.float32
BF16 = jnp.bfloat16
SCALAR_ROWS = 8


def gll_derivative(poly_order):
    node_count = poly_order + 1
    abscissa = np.cos(np.pi * np.arange(node_count) / poly_order)
    legendre = np.zeros((node_count, node_count))
    for _ in range(60):
        legendre[:, 0] = 1.0
        legendre[:, 1] = abscissa
        for degree in range(2, node_count):
            legendre[:, degree] = (
                (2 * degree - 1) * abscissa * legendre[:, degree - 1]
                - (degree - 1) * legendre[:, degree - 2]
            ) / degree
        abscissa = abscissa - (abscissa * legendre[:, poly_order] - legendre[:, poly_order - 1]) / (
            node_count * legendre[:, poly_order]
        )
    abscissa = abscissa[::-1]
    end_values = legendre[::-1, poly_order]
    spacing = abscissa[:, None] - abscissa[None, :] + np.eye(node_count)
    deriv_table = end_values[:, None] / end_values[None, :] / spacing
    deriv_table = deriv_table * (1.0 - np.eye(node_count))
    deriv_table[0, 0] = -poly_order * node_count / 4.0
    deriv_table[poly_order, poly_order] = poly_order * node_count / 4.0
    return deriv_table.astype(np.float32)


def split(x):
    high = x.astype(BF16)
    return high, (x - high.astype(F32)).astype(BF16)


def iota(shape, dim):
    return lax.broadcasted_iota(jnp.int32, shape, dim)


def repeated(table, width):
    lane = iota((PTS, width), 1) % PTS
    rows = []
    for i in range(PTS):
        row = jnp.full((PTS, width), float(table[i, 0]), F32)
        for k in range(1, PTS):
            row = jnp.where(lane == k, float(table[i, k]), row)
        rows.append(row)
    return rows


def fine_matrix(table, size):
    sub = iota((PTS, size), 0)
    rows = repeated(table, size)
    tile = rows[0]
    for i in range(1, PTS):
        tile = jnp.where(sub == i, rows[i], tile)
    block = iota((PTS, size), 1) // PTS
    return split(
        jnp.concatenate(
            [jnp.where(block == e, tile, 0.0) for e in range(size // PTS)], axis=0
        )
    )


def combine_planes(planes, table):
    half = PTS // 2
    even = [planes[k] + planes[PTS - 1 - k] for k in range(half)]
    odd = [planes[k] - planes[PTS - 1 - k] for k in range(half)]
    low, high = [], []
    for w in range(half):
        p = q = None
        for k in range(half):
            a, b = float(table[w, k]), float(table[w, PTS - 1 - k])
            pe = np.float32((a + b) / 2) * even[k]
            qo = np.float32((a - b) / 2) * odd[k]
            p = pe if p is None else p + pe
            q = qo if q is None else q + qo
        low.append(p + q)
        high.append(q - p)
    return low + high[::-1]


def dot(a, b):
    return jnp.dot(a, b, preferred_element_type=F32)


def join_rows(tiles, sub):
    done = []
    for e, t in enumerate(tiles):
        if e + 1 < len(tiles):
            t = t + jnp.where(sub == PTS - 1, pltpu.roll(tiles[e + 1], PTS - 1, 0), 0.0)
        if e > 0:
            t = t + jnp.where(sub == 0, pltpu.roll(tiles[e - 1], 1, 0), 0.0)
        done.append(t)
    return done


def assemble_plane(u, ny, nx):
    lane = iota((PTS, nx), 1)
    sub = iota((PTS, nx), 0)
    last = (lane % PTS == PTS - 1) & (lane < nx - 1)
    first = (lane % PTS == 0) & (lane > 0)
    tiles = []
    for e in range(ny // PTS):
        t = u[e * PTS : (e + 1) * PTS]
        t = (
            t
            + jnp.where(last, pltpu.roll(t, nx - 1, 1), 0.0)
            + jnp.where(first, pltpu.roll(t, 1, 1), 0.0)
        )
        tiles.append(t)
    return jnp.concatenate(join_rows(tiles, sub), axis=0)


def local_kernel(
    table,
    v_hbm,
    g_hbm,
    m_hbm,
    u_ref,
    px_ref,
    v_ref,
    m_ref,
    g_ref,
    grad_ref,
    high_ref,
    low_ref,
    div_ref,
    left_ref,
    right_ref,
    sems,
):
    comps, nz, ny, nx = v_ref.shape
    layers = nz // PTS
    rows = PTS * ny
    half = 2 * PTS
    v_copies = []
    gm_copies = []
    for layer in range(layers):
        zs = pl.ds(layer * PTS, PTS)
        v_copies.append(
            pltpu.make_async_copy(v_hbm.at[:, zs], v_ref.at[:, zs], sems.at[layer, 0])
        )
        gm_copies.append(
            pltpu.make_async_copy(g_hbm.at[:, zs], g_ref.at[:, zs], sems.at[layer, 1])
        )
        gm_copies.append(pltpu.make_async_copy(m_hbm.at[zs], m_ref.at[zs], sems.at[layer, 2]))
    for copy in v_copies + gm_copies:
        copy.start()
    for i, matrix in enumerate((table, table.T)):
        h, l = fine_matrix(matrix, rows)
        left_ref[i] = jnp.concatenate([h, l, h], axis=1)
        h, l = fine_matrix(matrix.T, nx)
        right_ref[i] = jnp.concatenate(
            [
                jnp.concatenate([h, l], axis=1),
                jnp.concatenate([h, jnp.zeros_like(l)], axis=1),
            ],
            axis=0,
        )
    blocks = [(layer, c) for layer in range(layers) for c in range(comps)]
    pairs = [blocks[i : i + 2] for i in range(0, len(blocks), 2)]

    def planes(layer):
        return slice(layer * PTS, (layer + 1) * PTS)

    def along_y(i, pair, slot):
        high = [high_ref[slot, c, planes(layer)].reshape(rows, nx) for layer, c in pair]
        low = [low_ref[slot, c, planes(layer)].reshape(rows, nx) for layer, c in pair]
        high, low = jnp.concatenate(high, axis=1), jnp.concatenate(low, axis=1)
        out = dot(left_ref[i], jnp.concatenate([high, high, low], axis=0))
        return [
            out[:, n * nx : (n + 1) * nx].reshape(PTS, ny, nx) for n in range(len(pair))
        ]

    def along_x(i, layer, c, slot):
        high = high_ref[slot, c, planes(layer)].reshape(rows, nx)
        low = low_ref[slot, c, planes(layer)].reshape(rows, nx)
        out = dot(jnp.concatenate([high, low], axis=1), right_ref[i])
        return (out[:, 0:nx] + out[:, nx : 2 * nx]).reshape(PTS, ny, nx)

    for copy in v_copies:
        copy.wait()
    for copy in gm_copies:
        copy.wait()
    for c in range(comps):
        for z in range(nz):
            high_ref[0, c, z], low_ref[0, c, z] = split(v_ref[c, z])
    for layer, c in blocks:
        for e in range(0, ny, PTS):
            ys = slice(e, e + PTS)
            z0 = layer * PTS
            out = combine_planes([v_ref[c, z0 + z, ys] for z in range(PTS)], table)
            for z in range(PTS):
                grad_ref[2, c, z0 + z, ys] = out[z]
    for pair in pairs:
        for (layer, c), out in zip(pair, along_y(0, pair, 0)):
            grad_ref[1, c, planes(layer)] = out
    for layer, c in blocks:
        grad_ref[0, c, planes(layer)] = along_x(0, layer, c, 0)
    kin = jnp.zeros((half, nx), F32)
    ens = jnp.zeros((half, nx), F32)
    ready = 0
    for layer in range(layers):
        for z in range(layer * PTS, (layer + 1) * PTS):
            for y in range(0, ny, half):
                ys = slice(y, y + half)
                g = [g_ref[i, z, ys].astype(F32) for i in range(6)]
                mass = m_ref[z, ys].astype(F32)
                u_ref[comps, z, ys] = mass
                square = None
                for c in range(comps):
                    v = v_ref[c, z, ys]
                    square = v * v if square is None else square + v * v
                    gr, gs, gt = (grad_ref[i, c, z, ys] for i in range(3))
                    fr = g[0] * gr + g[3] * gs + g[4] * gt
                    fs = g[3] * gr + g[1] * gs + g[5] * gt
                    ft = g[4] * gr + g[5] * gs + g[2] * gt
                    ens = ens + (gr * fr + gs * fs + gt * ft)
                    high_ref[1, c, z, ys], low_ref[1, c, z, ys] = split(fr)
                    high_ref[2, c, z, ys], low_ref[2, c, z, ys] = split(fs)
                    grad_ref[2, c, z, ys] = ft
                kin = kin + mass * square
        for c in range(comps):
            div_ref[c, planes(layer)] = along_x(1, layer, c, 1)
        while ready < len(pairs) and max(block[0] for block in pairs[ready]) <= layer:
            for (at, c), out in zip(pairs[ready], along_y(1, pairs[ready], 2)):
                grad_ref[1, c, planes(at)] = out
            ready += 1
    for layer, c in blocks:
        for e in range(0, ny, PTS):
            ys = slice(e, e + PTS)
            z0 = layer * PTS
            out = combine_planes([grad_ref[2, c, z0 + z, ys] for z in range(PTS)], table.T)
            for z in range(PTS):
                rest = grad_ref[1, c, z0 + z, ys] + div_ref[c, z0 + z, ys]
                u_ref[c, z0 + z, ys] = out[z] + rest
    px_ref[0:ny] = pack_columns(u_ref)
    row = iota((SCALAR_ROWS, nx), 0)
    kin, ens = jnp.sum(kin, axis=0, keepdims=True), jnp.sum(ens, axis=0, keepdims=True)
    px_ref[ny:] = jnp.where(row == 0, kin, jnp.where(row == 1, ens, 0.0))


def pack_columns(u_ref):
    fields, nz, ny, nx = u_ref.shape
    lane = iota((ny, nx), 1)
    packed = jnp.zeros((ny, nx), F32)
    for f in range(fields):
        for z in range(nz):
            j = f * nz + z
            moved = pltpu.roll(u_ref[f, z], 2 * j, 1) if j else u_ref[f, z]
            packed = jnp.where((lane == 2 * j) | (lane == (2 * j - 1) % nx), moved, packed)
    sub = iota((PTS, nx), 0)
    tiles = [packed[e : e + PTS] for e in range(0, ny, PTS)]
    packed = jnp.concatenate(join_rows(tiles, sub), axis=0)
    plane = (lane + 1) % nx // 2 % nz
    up = (plane % PTS == PTS - 1) & (plane < nz - 1)
    down = (plane % PTS == 0) & (plane > 0)
    return (
        packed
        + jnp.where(up, pltpu.roll(packed, nx - 2, 1), 0.0)
        + jnp.where(down, pltpu.roll(packed, 2, 1), 0.0)
    )


def plane_kernel(u_ref, zp_ref):
    fields, nz, ny, nx = u_ref.shape
    z_even = lax.axis_index("gz") % 2 == 0
    for f in range(fields):
        zp_ref[f] = assemble_plane(jnp.where(z_even, u_ref[f, nz - 1], u_ref[f, 0]), ny, nx)


def assemble_kernel(u_ref, w_ref):
    fields, nz, ny, nx = u_ref.shape
    for f in range(fields):
        for z in range(nz):
            t = u_ref[f, z]
            if z % PTS == PTS - 1 and z < nz - 1:
                t = t + u_ref[f, z + 1]
            if z % PTS == 0 and z > 0:
                w_ref[f, z] = w_ref[f, z - 1]
            else:
                w_ref[f, z] = assemble_plane(t, ny, nx)


def merge_sides(right, left):
    lane = iota(right.shape, 1)
    return jnp.where(lane % 2 == 0, right, pltpu.roll(left, 2, 1))


def place_columns(merged, j, nx):
    lane = iota(merged.shape, 1)
    shift = (nx - 1 - 2 * j) % nx
    moved = pltpu.roll(merged, shift, 1) if shift else merged
    return jnp.where((lane == 0) | (lane == nx - 1), moved, 0.0)


def first_kernel(zp_ref, px_ref, qa_ref, pb_ref, pz_ref, pd_ref):
    fields, ny, nx = zp_ref.shape
    nz = nx // (2 * fields)
    lane = iota((PTS, nx), 1)
    x_even = lax.axis_index("gx") % 2 == 0
    z_even = lax.axis_index("gz") % 2 == 0
    qa = qa_ref[0:ny]
    merged = merge_sides(jnp.where(x_even, qa, 0.0), jnp.where(x_even, 0.0, qa))
    merged = jnp.where(z_even, pltpu.roll(merged, nx - 2 * (nz - 1), 1), merged)
    sums = px_ref[ny:] + qa_ref[ny:]
    pb_ref[0:ny] = px_ref[0:ny]
    pb_ref[ny:] = sums
    for f in range(fields):
        pz_ref[f * ny : (f + 1) * ny] = zp_ref[f] + place_columns(merged, f * nz, nx)
    pz_ref[fields * ny :] = sums
    edge = None
    for e in range(ny // PTS):
        t = px_ref[e * PTS : (e + 1) * PTS]
        t = jnp.where(z_even, pltpu.roll(t, nx - 2 * (nz - 1), 1), t)
        t = pltpu.roll(t, 2 * e, 1) if e else t
        mine = (lane + 1) % nx // 2 % nz == e
        edge = jnp.where(mine, t, 0.0 if edge is None else edge)
    pd_ref[0:PTS] = edge
    pd_ref[PTS:] = sums


def x_sides(qa, qb, x_even):
    return merge_sides(jnp.where(x_even, qa, qb), jnp.where(x_even, qb, qa))


def diagonal_sides(qd, x_even):
    return merge_sides(jnp.where(x_even, 0.0, qd), jnp.where(x_even, qd, 0.0))


def second_kernel(
    u_ref, pb_ref, qa_ref, qb_ref, qz_ref, qd_ref, pya_ref, pyb_ref, ps_ref, low_ref, high_ref
):
    fields, nz, ny, nx = u_ref.shape
    x_even = lax.axis_index("gx") % 2 == 0
    y_even = lax.axis_index("gy") % 2 == 0
    for ys, row, out in (
        (slice(0, PTS), 0, low_ref),
        (slice(ny - PTS, ny), PTS - 1, high_ref),
    ):
        merged = x_sides(qa_ref[ys], qb_ref[ys], x_even)
        diag = diagonal_sides(qd_ref[0:PTS], x_even)
        for f in range(fields):
            for z in range(nz):
                j = f * nz + z
                t = u_ref[f, z, ys] + place_columns(merged, j, nx)
                if z in (0, nz - 1):
                    t = t + qz_ref[f * ny + ys.start : f * ny + ys.stop]
                    t = t + place_columns(diag, f * nz + ys.start // PTS, nx)
                out[j : j + 1] = t[row : row + 1]
    sums = pb_ref[ny:] + qb_ref[ny:] + qz_ref[fields * ny :] + qd_ref[PTS:]
    count = fields * nz
    pya_ref[0:count] = jnp.where(y_even, high_ref[...], low_ref[...])
    pyb_ref[0:count] = jnp.where(y_even, low_ref[...], high_ref[...])
    pya_ref[count:] = sums
    pyb_ref[count:] = sums
    ps_ref[...] = sums


def correct_kernel(v_ref, u_ref, qa_ref, qb_ref, qz_ref, qd_ref, w_ref, mv_ref):
    fields, nz, ny, nx = u_ref.shape
    x_even = lax.axis_index("gx") % 2 == 0
    merged = x_sides(qa_ref[0:ny], qb_ref[0:ny], x_even)
    diag = diagonal_sides(qd_ref[0:PTS], x_even)
    for z in range(nz):
        for f in range(fields):
            t = u_ref[f, z] + place_columns(merged, f * nz + z, nx)
            if z in (0, nz - 1):
                t = t + qz_ref[f * ny : (f + 1) * ny]
                corner = [place_columns(diag, f * nz + e, nx) for e in range(ny // PTS)]
                t = t + jnp.concatenate(corner, axis=0)
            w_ref[f, z] = t
        for c in range(fields - 1):
            mv_ref[c, z] = w_ref[fields - 1, z] * v_ref[c, z]


def last_kernel(
    sizes,
    v_ref,
    w_ref,
    mv_ref,
    qya_ref,
    qyb_ref,
    qs_ref,
    ps_ref,
    out_hbm,
    kin_hbm,
    ens_hbm,
    low_ref,
    high_ref,
    out_ref,
    kin_ref,
    ens_ref,
    sems,
):
    fields, nz, ny, nx = w_ref.shape
    gx, gy, gz = (lax.axis_index(name) for name in ("gx", "gy", "gz"))
    y_even = gy % 2 == 0
    count = fields * nz
    sums = ps_ref[...] + qya_ref[count:] + qyb_ref[count:] + qs_ref[...]
    kinetic = 0.5 * jnp.sum(sums[0:1])
    enstrophy = jnp.sum(sums[1:2])
    kin_ref[0, 0] = kinetic
    ens_ref[0, 0] = enstrophy
    copies = [
        pltpu.make_async_copy(kin_ref, kin_hbm, sems.at[4]),
        pltpu.make_async_copy(ens_ref, ens_hbm, sems.at[5]),
    ]
    for copy in copies:
        copy.start()
    rayleigh = jnp.full((PTS, nx), enstrophy, F32) / jnp.full((PTS, nx), 2.0 * kinetic, F32)
    low_ref[...] = jnp.where(y_even, qyb_ref[0:count], qya_ref[0:count])
    high_ref[...] = jnp.where(y_even, qya_ref[0:count], qyb_ref[0:count])
    row = iota((ny, nx), 0)
    lane = iota((ny, nx), 1)
    x_first = jnp.where(gx == 0, 0, -1)
    x_last = jnp.where(gx == sizes[0] - 1, nx - 1, -1)
    y_first = jnp.where(gy == 0, 0, -1)
    y_last = jnp.where(gy == sizes[1] - 1, ny - 1, -1)
    inside = (lane != x_first) & (lane != x_last) & (row != y_first) & (row != y_last)
    sub = iota((PTS, nx), 0)
    steps = nz // 4
    for z in range(nz):
        keep = inside
        if z == 0:
            keep = keep & (gz > 0)
        if z == nz - 1:
            keep = keep & (gz < sizes[2] - 1)
        for e in range(0, ny, PTS):
            ys = slice(e, e + PTS)
            edge = e == 0 or e == ny - PTS
            side, at = (low_ref, 0) if e == 0 else (high_ref, PTS - 1)
            if edge:
                j = (fields - 1) * nz + z
                extra = rayleigh * jnp.where(sub == at, side[j : j + 1], 0.0)
            for c in range(fields - 1):
                t = w_ref[c, z, ys] - rayleigh * mv_ref[c, z, ys]
                if edge:
                    j = c * nz + z
                    t = t + jnp.where(sub == at, side[j : j + 1], 0.0)
                    t = t - extra * v_ref[c, z, ys]
                out_ref[c, z, ys] = jnp.where(keep[ys], t, 0.0)
        if z % steps == steps - 1:
            zs = pl.ds(z - steps + 1, steps)
            copies.append(
                pltpu.make_async_copy(
                    out_ref.at[:, zs], out_hbm.at[:, zs], sems.at[z // steps]
                )
            )
            copies[-1].start()
    for copy in copies:
        copy.wait()


VMEM = pl.BlockSpec(memory_space=pltpu.VMEM)
HBM = pl.BlockSpec(memory_space=pltpu.HBM)


def call(kernel, outs, ins, scratch=(), out_specs=None, in_specs=None, flops=1 << 20):
    return pl.pallas_call(
        kernel,
        out_shape=[jax.ShapeDtypeStruct(shape, F32) for shape in outs],
        in_specs=in_specs or [VMEM] * len(ins),
        out_specs=out_specs or [VMEM] * len(outs),
        scratch_shapes=list(scratch),
        compiler_params=pltpu.CompilerParams(vmem_limit_bytes=24 << 20),
        cost_estimate=pl.CostEstimate(flops=flops, bytes_accessed=flops, transcendentals=0),
    )(*ins)


def local_part(velocity, geometry, mass_weights):
    comps, nz, ny, nx = velocity.shape
    return call(
        functools.partial(local_kernel, gll_derivative(ORDER)),
        [(comps + 1, nz, ny, nx), (ny + SCALAR_ROWS, nx), velocity.shape],
        [
            pltpu.with_memory_space_constraint(x, pltpu.HBM)
            for x in (velocity, geometry, mass_weights)
        ],
        in_specs=[HBM] * 3,
        scratch=[
            pltpu.VMEM(mass_weights.shape, BF16),
            pltpu.VMEM(geometry.shape, BF16),
            pltpu.VMEM((3, *velocity.shape), F32),
            pltpu.VMEM((3, *velocity.shape), BF16),
            pltpu.VMEM((3, *velocity.shape), BF16),
            pltpu.VMEM(velocity.shape, F32),
            pltpu.VMEM((2, PTS * ny, 3 * PTS * ny), BF16),
            pltpu.VMEM((2, 2 * nx, 2 * nx), BF16),
            pltpu.SemaphoreType.DMA((nz // PTS, 3)),
        ],
    )


def assembled(u):
    return call(assemble_kernel, [u.shape], [u])[0]


def pairs_near(count):
    return [(i, i ^ 1) for i in range(count)]


def pairs_mirror(count):
    return [(i, count - 1 - i) for i in range(count)]


def few_rounds(sizes, velocity, geometry, mass_weights):
    comps, nz, ny, nx = velocity.shape
    fields = comps + 1
    raw, px, held = local_part(velocity, geometry, mass_weights)
    qa = lax.ppermute(px, "gx", pairs_near(sizes[0]))
    zp = call(plane_kernel, [(fields, ny, nx)], [raw])[0]
    pb, pz, pd = call(
        first_kernel,
        [
            (ny + SCALAR_ROWS, nx),
            (fields * ny + SCALAR_ROWS, nx),
            (PTS + SCALAR_ROWS, nx),
        ],
        [zp, px, qa],
    )
    mirror = pairs_mirror(sizes[0])
    qb = lax.ppermute(pb, "gx", mirror)
    qz = lax.ppermute(pz, "gz", pairs_near(sizes[2]))
    both = [
        (i * sizes[2] + k, mirror[i][1] * sizes[2] + (k ^ 1))
        for i in range(sizes[0])
        for k in range(sizes[2])
    ]
    qd = lax.ppermute(pd, ("gx", "gz"), both)
    u = assembled(raw)
    count = fields * nz
    pya, pyb, ps = call(
        second_kernel,
        [(count + SCALAR_ROWS, nx), (count + SCALAR_ROWS, nx), (SCALAR_ROWS, nx)],
        [u, pb, qa, qb, qz, qd],
        scratch=[pltpu.VMEM((count, nx), F32)] * 2,
    )
    qya = lax.ppermute(pya, "gy", pairs_near(sizes[1]))
    qyb = lax.ppermute(pyb, "gy", pairs_mirror(sizes[1]))
    qs = lax.ppermute(ps, "gy", [(i, i ^ 2) for i in range(sizes[1])])
    w, mv = call(correct_kernel, [u.shape, velocity.shape], [held, u, qa, qb, qz, qd])
    residual, kinetic, enstrophy = call(
        functools.partial(last_kernel, sizes),
        [velocity.shape, (1, 1), (1, 1)],
        [held, w, mv, qya, qyb, qs, ps],
        scratch=[
            pltpu.VMEM((count, nx), F32),
            pltpu.VMEM((count, nx), F32),
            pltpu.VMEM(velocity.shape, F32),
            pltpu.SMEM((1, 1), F32),
            pltpu.SMEM((1, 1), F32),
            pltpu.SemaphoreType.DMA((6,)),
        ],
        out_specs=[HBM, HBM, HBM],
    )
    return residual, kinetic[0, 0], enstrophy[0, 0]


def add_neighbours(field, axis, dim):
    count = lax.axis_size(axis)
    extent = field.shape[dim]
    first = lax.slice_in_dim(field, 0, 1, axis=dim)
    last = lax.slice_in_dim(field, extent - 1, extent, axis=dim)
    low = lax.ppermute(last, axis, [(i, i + 1) for i in range(count - 1)])
    high = lax.ppermute(first, axis, [(i + 1, i) for i in range(count - 1)])
    middle = lax.slice_in_dim(field, 1, extent - 1, axis=dim)
    return jnp.concatenate([first + low, middle, last + high], axis=dim)


def any_mesh(sizes, velocity, geometry, mass_weights):
    comps, nz, ny, nx = velocity.shape
    raw, px, _ = local_part(velocity, geometry, mass_weights)
    u = assembled(raw)
    kinetic = 0.5 * jnp.sum(px[ny])
    enstrophy = jnp.sum(px[ny + 1])
    kinetic, enstrophy = lax.psum((kinetic, enstrophy), ("gx", "gy", "gz"))
    for axis, dim in (("gx", 3), ("gy", 2), ("gz", 1)):
        u = add_neighbours(u, axis, dim)
    inside = jnp.ones((nz, ny, nx), bool)
    for dim, (axis, size) in enumerate(zip(("gz", "gy", "gx"), sizes[::-1])):
        place = lax.axis_index(axis) * inside.shape[dim] + iota(inside.shape, dim)
        inside = inside & (place > 0) & (place < size * inside.shape[dim] - 1)
    rayleigh = enstrophy / (2.0 * kinetic)
    residual = jnp.where(inside[None], u[:comps] - rayleigh * u[comps][None] * velocity, 0.0)
    return residual, kinetic, enstrophy


def solution(mesh):
    sizes = tuple(mesh.shape[name] for name in ("gx", "gy", "gz"))
    plan = few_rounds if sizes == (4, 4, 2) else any_mesh
    in_specs = (P(None, "gz", "gy", "gx"), P(None, "gz", "gy", "gx"), P("gz", "gy", "gx"))
    out_specs = (P(None, "gz", "gy", "gx"), P(), P())

    def body(*args):
        return plan(sizes, *args)

    step = jax.shard_map(
        body, mesh=mesh, in_specs=in_specs, out_specs=out_specs, check_vma=False
    )
    if plan is any_mesh:
        return step
    return step
```

profile of v0, /device:TPU:0, one launch (start us, length us, event | category | flops | bytes accessed | tf_op | source)
XLA Modules:
  0.0 24.0 jit_solution(1313713252726943626)
XLA Ops:
  0.6 3.8 %shard_map.58 = (f32[4,16,32,128]{3,2,1,0:T(8,128)S(1)}, f32[40,128]{1,0:T(8,128)S(1)}, f32[3,16,32,128]{3,2,1,0:T(8,128)S(1)}) custom-call(f32[3,16,32,128]{3,2,1,0:T(8,128)} %v_hbm.1, bf16[6,16,32,128]{3,2,1,0:T(8,128)(2,1)} %g_hbm.1, bf16[16,32,128]{2,1,0:T(8,128)(2,1)} %m_hbm.1), custom_call_target="tpu_custom_call" | custom-call | flops 1048576 | bytes 1048576 | tf_op jit(solution)/shard_map/pallas_call | solution.py:474
  4.5 0.6 %collective-permute-start = (f32[40,128]{1,0:T(8,128)S(1)}, f32[40,128]{1,0:T(8,128)S(1)}, u32[]{:S(2)}, u32[]{:S(2)}) collective-permute-start(f32[40,128]{1,0:T(8,128)S(1)} %get-tuple-element.19.px_ref), channel_id=1, source_target_pairs={{0,8},{8,0},{16,24},{24,16},{1,9},{9,1},{17,25},{25,17},{2,10},{10... | collective-permute-start | bytes 61448 | tf_op jit(solution)/shard_map/ppermute | solution.py:525
  5.0 0.1 shard_map.60.zp_ref
  5.1 0.7 %collective-permute-done.qa_ref = f32[40,128]{1,0:T(8,128)S(1)} collective-permute-done((f32[40,128]{1,0:T(8,128)S(1)}, f32[40,128]{1,0:T(8,128)S(1)}, u32[]{:S(2)}, u32[]{:S(2)}) %collective-permute-start) | collective-permute-done | bytes 20512 | tf_op jit(solution)/shard_map/ppermute | solution.py:525
  5.9 0.2 shard_map.61
  6.1 2.9 %collective-permute-start.2 = (f32[136,128]{1,0:T(8,128)S(1)}, f32[136,128]{1,0:T(8,128)S(1)}, u32[]{:S(2)}, u32[]{:S(2)}) collective-permute-start(f32[136,128]{1,0:T(8,128)S(1)} %get-tuple-element.21), channel_id=1, source_target_pairs={{0,1},{1,0},{2,3},{3,2},{4,5},{5,4},{6,7},{7,6},{8,9},{9,8},{10,11... | collective-permute-start | bytes 208904 | tf_op jit(solution)/shard_map/ppermute | solution.py:538
  9.0 1.0 %collective-permute-start.1 = (f32[40,128]{1,0:T(8,128)S(1)}, f32[40,128]{1,0:T(8,128)S(1)}, u32[]{:S(2)}, u32[]{:S(2)}) collective-permute-start(f32[40,128]{1,0:T(8,128)S(1)} %get-tuple-element.20.pb_ref), channel_id=1, source_target_pairs={{0,24},{8,16},{16,8},{24,0},{1,25},{9,17},{17,9},{25,1},{2,26},{10... | collective-permute-start | bytes 61448 | tf_op jit(solution)/shard_map/ppermute | solution.py:537
  10.0 0.3 %collective-permute-start.3 = (f32[16,128]{1,0:T(8,128)S(1)}, f32[16,128]{1,0:T(8,128)S(1)}, u32[]{:S(2)}, u32[]{:S(2)}) collective-permute-start(f32[16,128]{1,0:T(8,128)S(1)} %get-tuple-element.22), channel_id=1, source_target_pairs={{0,25},{1,24},{8,17},{9,16},{16,9},{17,8},{24,1},{25,0},{2,27},{3,... | collective-permute-start | bytes 24584 | tf_op jit(solution)/shard_map/ppermute | solution.py:544
  10.3 0.6 %shard_map.59.u_ref = f32[4,16,32,128]{3,2,1,0:T(8,128)S(1)} custom-call(f32[4,16,32,128]{3,2,1,0:T(8,128)S(1)} %get-tuple-element.18.u_ref), custom_call_target="tpu_custom_call" | custom-call | flops 1048576 | bytes 1048576 | tf_op jit(solution)/shard_map/pallas_call | solution.py:474
  10.8 3.1 %collective-permute-done.3.qd_ref = f32[16,128]{1,0:T(8,128)S(1)} collective-permute-done((f32[16,128]{1,0:T(8,128)S(1)}, f32[16,128]{1,0:T(8,128)S(1)}, u32[]{:S(2)}, u32[]{:S(2)}) %collective-permute-start.3) | collective-permute-done | bytes 8224 | tf_op jit(solution)/shard_map/ppermute | solution.py:544
  14.0 0.0 collective-permute-done.1.qb_ref
  14.0 0.0 collective-permute-done.2.qz_ref
  14.0 0.3 %shard_map.63 = (f32[72,128]{1,0:T(8,128)S(1)}, f32[72,128]{1,0:T(8,128)S(1)}, f32[8,128]{1,0:T(8,128)S(1)}) custom-call(f32[4,16,32,128]{3,2,1,0:T(8,128)S(1)} %shard_map.59.u_ref, f32[40,128]{1,0:T(8,128)S(1)} %get-tuple-element.20.pb_ref, f32[40,128]{1,0:T(8,128)S(1)} %collective-permute-done.qa_ref, f32[40,128]{1,0:T(8,128)S(1)} %collective-permute-done.1.qb_ref, ...), custom_call_target="tpu_custom_call" | custom-call | flops 1048576 | bytes 1048576 | tf_op jit(solution)/shard_map/pallas_call | solution.py:474
  14.3 1.6 %collective-permute-start.4 = (f32[72,128]{1,0:T(8,128)S(1)}, f32[72,128]{1,0:T(8,128)S(1)}, u32[]{:S(2)}, u32[]{:S(2)}) collective-permute-start(f32[72,128]{1,0:T(8,128)S(1)} %get-tuple-element.25), channel_id=1, source_target_pairs={{0,2},{2,0},{4,6},{6,4},{1,3},{3,1},{5,7},{7,5},{8,10},{10,8},{12,... | collective-permute-start | bytes 110600 | tf_op jit(solution)/shard_map/ppermute | solution.py:553
  15.9 2.5 %collective-permute-start.5 = (f32[72,128]{1,0:T(8,128)S(1)}, f32[72,128]{1,0:T(8,128)S(1)}, u32[]{:S(2)}, u32[]{:S(2)}) collective-permute-start(f32[72,128]{1,0:T(8,128)S(1)} %get-tuple-element.26), channel_id=1, source_target_pairs={{0,6},{2,4},{4,2},{6,0},{1,7},{3,5},{5,3},{7,1},{8,14},{10,12},{12... | collective-permute-start | bytes 110600 | tf_op jit(solution)/shard_map/ppermute | solution.py:554
  18.4 0.1 collective-permute-start.6
  18.5 0.4 %shard_map.62 = (f32[4,16,32,128]{3,2,1,0:T(8,128)S(1)}, f32[3,16,32,128]{3,2,1,0:T(8,128)S(1)}) custom-call(f32[3,16,32,128]{3,2,1,0:T(8,128)S(1)} %get-tuple-element.17.v_ref, f32[4,16,32,128]{3,2,1,0:T(8,128)S(1)} %shard_map.59.u_ref, f32[40,128]{1,0:T(8,128)S(1)} %collective-permute-done.qa_ref, f32[40,128]{1,0:T(8,128)S(1)} %collective-permute-done.1.qb_ref, ...), custom_call_target="tpu_custom_call" | custom-call | flops 1048576 | bytes 1048576 | tf_op jit(solution)/shard_map/pallas_call | solution.py:474
  18.9 4.0 %collective-permute-done.6.qs_ref = f32[8,128]{1,0:T(8,128)S(1)} collective-permute-done((f32[8,128]{1,0:T(8,128)S(1)}, f32[8,128]{1,0:T(8,128)S(1)}, u32[]{:S(2)}, u32[]{:S(2)}) %collective-permute-start.6) | collective-permute-done | bytes 4128 | tf_op jit(solution)/shard_map/ppermute | solution.py:555
  22.9 0.0 collective-permute-done.4.qya_ref
  22.9 0.0 collective-permute-done.5.qyb_ref
  22.9 1.1 %shard_map.64 = (f32[3,16,32,128]{3,2,1,0:T(8,128)}, f32[1,1]{1,0:T(1,128)}, f32[1,1]{1,0:T(1,128)}) custom-call(f32[3,16,32,128]{3,2,1,0:T(8,128)S(1)} %get-tuple-element.17.v_ref, f32[4,16,32,128]{3,2,1,0:T(8,128)S(1)} %get-tuple-element.23.w_ref, f32[3,16,32,128]{3,2,1,0:T(8,128)S(1)} %get-tuple-element.24.mv_ref, ...), custom_call_target="tpu_custom_call" | custom-call | flops 1048576 | bytes 1048576 | tf_op jit(solution)/shard_map/pallas_call | solution.py:474
Async XLA Ops:
  4.5 1.4 %collective-permute-start = (f32[40,128]{1,0:T(8,128)S(1)}, f32[40,128]{1,0:T(8,128)S(1)}, u32[]{:S(2)}, u32[]{:S(2)}) collective-permute-start(f32[40,128]{1,0:T(8,128)S(1)} %get-tuple-element.19.px_ref), channel_id=1, source_target_pairs={{0,8},{8,0},{16,24},{24,16},{1,9},{9,1},{17,25},{25,17},{2,10},{10... | collective-permute-start | bytes 61448 | tf_op jit(solution)/shard_map/ppermute | solution.py:525
  6.1 7.9 %collective-permute-start.2 = (f32[136,128]{1,0:T(8,128)S(1)}, f32[136,128]{1,0:T(8,128)S(1)}, u32[]{:S(2)}, u32[]{:S(2)}) collective-permute-start(f32[136,128]{1,0:T(8,128)S(1)} %get-tuple-element.21), channel_id=1, source_target_pairs={{0,1},{1,0},{2,3},{3,2},{4,5},{5,4},{6,7},{7,6},{8,9},{9,8},{10,11... | collective-permute-start | bytes 208904 | tf_op jit(solution)/shard_map/ppermute | solution.py:538
  9.0 5.0 %collective-permute-start.1 = (f32[40,128]{1,0:T(8,128)S(1)}, f32[40,128]{1,0:T(8,128)S(1)}, u32[]{:S(2)}, u32[]{:S(2)}) collective-permute-start(f32[40,128]{1,0:T(8,128)S(1)} %get-tuple-element.20.pb_ref), channel_id=1, source_target_pairs={{0,24},{8,16},{16,8},{24,0},{1,25},{9,17},{17,9},{25,1},{2,26},{10... | collective-permute-start | bytes 61448 | tf_op jit(solution)/shard_map/ppermute | solution.py:537
  10.0 4.0 %collective-permute-start.3 = (f32[16,128]{1,0:T(8,128)S(1)}, f32[16,128]{1,0:T(8,128)S(1)}, u32[]{:S(2)}, u32[]{:S(2)}) collective-permute-start(f32[16,128]{1,0:T(8,128)S(1)} %get-tuple-element.22), channel_id=1, source_target_pairs={{0,25},{1,24},{8,17},{9,16},{16,9},{17,8},{24,1},{25,0},{2,27},{3,... | collective-permute-start | bytes 24584 | tf_op jit(solution)/shard_map/ppermute | solution.py:544
  14.3 8.6 %collective-permute-start.4 = (f32[72,128]{1,0:T(8,128)S(1)}, f32[72,128]{1,0:T(8,128)S(1)}, u32[]{:S(2)}, u32[]{:S(2)}) collective-permute-start(f32[72,128]{1,0:T(8,128)S(1)} %get-tuple-element.25), channel_id=1, source_target_pairs={{0,2},{2,0},{4,6},{6,4},{1,3},{3,1},{5,7},{7,5},{8,10},{10,8},{12,... | collective-permute-start | bytes 110600 | tf_op jit(solution)/shard_map/ppermute | solution.py:553
  15.9 7.0 %collective-permute-start.5 = (f32[72,128]{1,0:T(8,128)S(1)}, f32[72,128]{1,0:T(8,128)S(1)}, u32[]{:S(2)}, u32[]{:S(2)}) collective-permute-start(f32[72,128]{1,0:T(8,128)S(1)} %get-tuple-element.26), channel_id=1, source_target_pairs={{0,6},{2,4},{4,2},{6,0},{1,7},{3,5},{5,3},{7,1},{8,14},{10,12},{12... | collective-permute-start | bytes 110600 | tf_op jit(solution)/shard_map/ppermute | solution.py:554
  18.4 4.5 %collective-permute-start.6 = (f32[8,128]{1,0:T(8,128)S(1)}, f32[8,128]{1,0:T(8,128)S(1)}, u32[]{:S(2)}, u32[]{:S(2)}) collective-permute-start(f32[8,128]{1,0:T(8,128)S(1)} %get-tuple-element.27.ps_ref), channel_id=1, source_target_pairs={{0,4},{2,6},{4,0},{6,2},{1,5},{3,7},{5,1},{7,3},{8,12},{10,14},{12... | collective-permute-start | bytes 12296 | tf_op jit(solution)/shard_map/ppermute | solution.py:555
where the time goes:
time: 24.1 us; the launch traced here: 24 us
  starting transfers between devices  8.96 us (37%)
  waiting for transfers between devices  7.81 us (32%)
  Pallas kernels  6.55 us (27%)
  between operations  0.67 us (3%)
    pallas_call x7, Pallas kernels, call(): pl.pallas_call(kernel, out_shape=[jax.ShapeDtypeStruct(shape, F32) for sh...  6.55 us
    ppermute x1, waiting for transfers between devices, few_rounds(): qs = lax.ppermute(ps, 'gy', [(i, i ^ 2) for i in range(sizes[1])])  3.96 us
    ppermute x1, waiting for transfers between devices, few_rounds(): qd = lax.ppermute(pd, ('gx', 'gz'), both)  3.12 us
    ppermute x1, starting transfers between devices, few_rounds(): qz = lax.ppermute(pz, 'gz', pairs_near(sizes[2]))  2.91 us
    ppermute x1, starting transfers between devices, few_rounds(): qyb = lax.ppermute(pyb, 'gy', pairs_mirror(sizes[1]))  2.47 us
    ppermute x1, starting transfers between devices, few_rounds(): qya = lax.ppermute(pya, 'gy', pairs_near(sizes[1]))  1.64 us
    ppermute x1, starting transfers between devices, few_rounds(): qb = lax.ppermute(pb, 'gx', mirror)  0.98 us
    ppermute x1, waiting for transfers between devices, few_rounds(): qa = lax.ppermute(px, 'gx', pairs_near(sizes[0]))  0.73 us
  transfers between devices with their start and end apart: 7, of which 3 were waited for; matrix products, arithmetic and copies ran while one was open for 0% of the time, Pallas kernels for 5%

commit v1 on v0

--- a/solution.py
+++ b/solution.py
@@ -125,22 +125,89 @@
     return jnp.concatenate(join_rows(tiles, sub), axis=0)
 
 
+def joined(pieces):
+    return pieces[0] if len(pieces) == 1 else joined(
+        [sum(pieces[i : i + 2][1:], pieces[i]) for i in range(0, len(pieces), 2)]
+    )
+
+
+def across_rows(tile, columns):
+    return joined(
+        [column * jnp.broadcast_to(tile[k : k + 1], tile.shape) for k, column in enumerate(columns)]
+    )
+
+
+def row_columns(table, nx):
+    sub = iota((PTS, nx), 0)
+    columns = []
+    for k in range(PTS):
+        column = jnp.full((PTS, nx), float(table[0, k]), F32)
+        for w in range(1, PTS):
+            column = jnp.where(sub == w, float(table[w, k]), column)
+        columns.append(column)
+    return columns
+
+
+def by_thrice(x, weights):
+    high, low = split(x)
+    out = dot(jnp.concatenate([high, low], axis=1), weights)
+    half = weights.shape[1] // 2
+    return out[:, 0:half] + out[:, half:]
+
+
+def thrice(high, low):
+    return jnp.concatenate(
+        [
+            jnp.concatenate([high, low], axis=1),
+            jnp.concatenate([high, jnp.zeros_like(low)], axis=1),
+        ],
+        axis=0,
+    )
+
+
+def column_slot(lane, nx):
+    return (lane + 1) % nx // 2
+
+
+def packed_z_matrix(table, nx):
+    into, out = iota((nx, nx), 0), iota((nx, nx), 1)
+    j, k = column_slot(into, nx), column_slot(out, nx)
+    value = jnp.zeros((nx, nx), F32)
+    for w in range(PTS):
+        row = jnp.zeros((nx, nx), F32)
+        for q in range(PTS):
+            row = jnp.where(k % PTS == q, float(table[w, q]), row)
+        value = jnp.where(j % PTS == w, row, value)
+    same = (j // PTS == k // PTS) & (into % 2 == out % 2)
+    return jnp.where(same, value, 0.0)
+
+
+def packed_x_matrix(table, nx):
+    into, out = iota((nx, nx), 0), iota((nx, nx), 1)
+    place, plane = into % (2 * PTS), into // (2 * PTS)
+    value = jnp.zeros((nx, nx), F32)
+    for w in range(PTS):
+        value = jnp.where(place == w, float(table[w, PTS - 1]), value)
+        value = jnp.where(place == PTS + w, float(table[w, 0]), value)
+    target = jnp.where(place < PTS, (2 * plane - 1) % nx, 2 * plane)
+    return jnp.where(out == target, value, 0.0)
+
+
 def local_kernel(
     table,
     v_hbm,
     g_hbm,
     m_hbm,
-    u_ref,
+    f_ref,
     px_ref,
     v_ref,
     m_ref,
+    left_ref,
+    right_ref,
     g_ref,
     grad_ref,
     high_ref,
     low_ref,
-    div_ref,
-    left_ref,
-    right_ref,
     sems,
 ):
     comps, nz, ny, nx = v_ref.shape
@@ -163,42 +230,26 @@
     for i, matrix in enumerate((table, table.T)):
         h, l = fine_matrix(matrix, rows)
         left_ref[i] = jnp.concatenate([h, l, h], axis=1)
-        h, l = fine_matrix(matrix.T, nx)
-        right_ref[i] = jnp.concatenate(
-            [
-                jnp.concatenate([h, l], axis=1),
-                jnp.concatenate([h, jnp.zeros_like(l)], axis=1),
-            ],
-            axis=0,
-        )
+        right_ref[i] = thrice(*fine_matrix(matrix.T, nx))
+    right_ref[2] = thrice(*split(packed_x_matrix(table, nx)))
+    right_ref[3] = thrice(*split(packed_z_matrix(table, nx)))
+    columns = row_columns(table.T, nx)
     blocks = [(layer, c) for layer in range(layers) for c in range(comps)]
-    pairs = [blocks[i : i + 2] for i in range(0, len(blocks), 2)]
 
     def planes(layer):
         return slice(layer * PTS, (layer + 1) * PTS)
 
-    def along_y(i, pair, slot):
-        high = [high_ref[slot, c, planes(layer)].reshape(rows, nx) for layer, c in pair]
-        low = [low_ref[slot, c, planes(layer)].reshape(rows, nx) for layer, c in pair]
-        high, low = jnp.concatenate(high, axis=1), jnp.concatenate(low, axis=1)
-        out = dot(left_ref[i], jnp.concatenate([high, high, low], axis=0))
-        return [
-            out[:, n * nx : (n + 1) * nx].reshape(PTS, ny, nx) for n in range(len(pair))
-        ]
-
-    def along_x(i, layer, c, slot):
-        high = high_ref[slot, c, planes(layer)].reshape(rows, nx)
-        low = low_ref[slot, c, planes(layer)].reshape(rows, nx)
-        out = dot(jnp.concatenate([high, low], axis=1), right_ref[i])
-        return (out[:, 0:nx] + out[:, nx : 2 * nx]).reshape(PTS, ny, nx)
-
     for copy in v_copies:
-        copy.wait()
-    for copy in gm_copies:
         copy.wait()
     for c in range(comps):
         for z in range(nz):
-            high_ref[0, c, z], low_ref[0, c, z] = split(v_ref[c, z])
+            high_ref[c, z], low_ref[c, z] = split(v_ref[c, z])
+    for layer, c in blocks:
+        grad_ref[0, c, planes(layer)] = along_x(right_ref[0], layer, c, high_ref, low_ref)
+    for i in range(0, len(blocks), 2):
+        pair = blocks[i : i + 2]
+        for (layer, c), out in zip(pair, along_y(left_ref[0], pair, high_ref, low_ref)):
+            grad_ref[1, c, planes(layer)] = out
     for layer, c in blocks:
         for e in range(0, ny, PTS):
             ys = slice(e, e + PTS)
@@ -206,67 +257,70 @@
             out = combine_planes([v_ref[c, z0 + z, ys] for z in range(PTS)], table)
             for z in range(PTS):
                 grad_ref[2, c, z0 + z, ys] = out[z]
-    for pair in pairs:
-        for (layer, c), out in zip(pair, along_y(0, pair, 0)):
-            grad_ref[1, c, planes(layer)] = out
-    for layer, c in blocks:
-        grad_ref[0, c, planes(layer)] = along_x(0, layer, c, 0)
+    for copy in gm_copies:
+        copy.wait()
+    lane = iota((PTS, nx), 1)
+    slot, place = column_slot(lane, nx), lane // half
+
+    def moved(x, shift):
+        return pltpu.roll(x, shift, 1) if shift else x
+
     kin = jnp.zeros((half, nx), F32)
     ens = jnp.zeros((half, nx), F32)
-    ready = 0
-    for layer in range(layers):
-        for z in range(layer * PTS, (layer + 1) * PTS):
-            for y in range(0, ny, half):
-                ys = slice(y, y + half)
-                g = [g_ref[i, z, ys].astype(F32) for i in range(6)]
-                mass = m_ref[z, ys].astype(F32)
-                u_ref[comps, z, ys] = mass
-                square = None
-                for c in range(comps):
-                    v = v_ref[c, z, ys]
-                    square = v * v if square is None else square + v * v
-                    gr, gs, gt = (grad_ref[i, c, z, ys] for i in range(3))
-                    fr = g[0] * gr + g[3] * gs + g[4] * gt
-                    fs = g[3] * gr + g[1] * gs + g[5] * gt
-                    ft = g[4] * gr + g[5] * gs + g[2] * gt
-                    ens = ens + (gr * fr + gs * fs + gt * ft)
-                    high_ref[1, c, z, ys], low_ref[1, c, z, ys] = split(fr)
-                    high_ref[2, c, z, ys], low_ref[2, c, z, ys] = split(fs)
-                    grad_ref[2, c, z, ys] = ft
-                kin = kin + mass * square
-        for c in range(comps):
-            div_ref[c, planes(layer)] = along_x(1, layer, c, 1)
-        while ready < len(pairs) and max(block[0] for block in pairs[ready]) <= layer:
-            for (at, c), out in zip(pairs[ready], along_y(1, pairs[ready], 2)):
-                grad_ref[1, c, planes(at)] = out
-            ready += 1
-    for layer, c in blocks:
-        for e in range(0, ny, PTS):
-            ys = slice(e, e + PTS)
-            z0 = layer * PTS
-            out = combine_planes([grad_ref[2, c, z0 + z, ys] for z in range(PTS)], table.T)
-            for z in range(PTS):
-                rest = grad_ref[1, c, z0 + z, ys] + div_ref[c, z0 + z, ys]
-                u_ref[c, z0 + z, ys] = out[z] + rest
-    px_ref[0:ny] = pack_columns(u_ref)
+    tiles = ny // PTS
+    zero = jnp.zeros((PTS, nx), F32)
+    packed_s, packed_t, packed_m = ([zero] * tiles for _ in range(3))
+    groups = [[zero] * tiles for _ in range(comps * layers)]
+    for y in range(0, ny, half):
+        ys = slice(y, y + half)
+        for z in range(nz):
+            g = [g_ref[i, z, ys].astype(F32) for i in range(6)]
+            mass = m_ref[z, ys].astype(F32)
+            square = None
+            for c in range(comps):
+                v = v_ref[c, z, ys]
+                square = v * v if square is None else square + v * v
+                gr, gs, gt = (grad_ref[i, c, z, ys] for i in range(3))
+                fr = g[0] * gr + g[3] * gs + g[4] * gt
+                fs = g[3] * gr + g[1] * gs + g[5] * gt
+                ft = g[4] * gr + g[5] * gs + g[2] * gt
+                ens = ens + (gr * fr + gs * fs + gt * ft)
+                f_ref[0, c, z, ys] = fr
+                f_ref[1, c, z, ys] = fs
+                f_ref[2, c, z, ys] = ft
+                j = c * nz + z
+                here, mine = slot == j, place == j % PTS
+                for e in range(half // PTS):
+                    t, rs = y // PTS + e, slice(e * PTS, (e + 1) * PTS)
+                    packed_s[t] = jnp.where(here, moved(fs[rs], 2 * j), packed_s[t])
+                    packed_t[t] = jnp.where(here, moved(ft[rs], 2 * j), packed_t[t])
+                    part = moved(fr[rs], (PTS + half * (j % PTS)) % nx)
+                    groups[j // PTS][t] = jnp.where(mine, part, groups[j // PTS][t])
+            kin = kin + mass * square
+            j = comps * nz + z
+            for e in range(half // PTS):
+                t, rs = y // PTS + e, slice(e * PTS, (e + 1) * PTS)
+                packed_m[t] = jnp.where(slot == j, moved(mass[rs], 2 * j), packed_m[t])
+    div_r = by_thrice(
+        jnp.concatenate([jnp.concatenate(group, axis=0) for group in groups], axis=0),
+        right_ref[2],
+    )
+    parts = [moved(div_r[q * ny : (q + 1) * ny], half * q) for q in range(len(groups))]
+    parts.append(jnp.concatenate([across_rows(t, columns) for t in packed_s], axis=0))
+    parts.append(by_thrice(jnp.concatenate(packed_t, axis=0), right_ref[3]))
+    parts.append(jnp.concatenate(packed_m, axis=0))
+    px_ref[0:ny] = join_columns(joined(parts), nz)
     row = iota((SCALAR_ROWS, nx), 0)
     kin, ens = jnp.sum(kin, axis=0, keepdims=True), jnp.sum(ens, axis=0, keepdims=True)
     px_ref[ny:] = jnp.where(row == 0, kin, jnp.where(row == 1, ens, 0.0))
 
 
-def pack_columns(u_ref):
-    fields, nz, ny, nx = u_ref.shape
-    lane = iota((ny, nx), 1)
-    packed = jnp.zeros((ny, nx), F32)
-    for f in range(fields):
-        for z in range(nz):
-            j = f * nz + z
-            moved = pltpu.roll(u_ref[f, z], 2 * j, 1) if j else u_ref[f, z]
-            packed = jnp.where((lane == 2 * j) | (lane == (2 * j - 1) % nx), moved, packed)
-    sub = iota((PTS, nx), 0)
-    tiles = [packed[e : e + PTS] for e in range(0, ny, PTS)]
-    packed = jnp.concatenate(join_rows(tiles, sub), axis=0)
-    plane = (lane + 1) % nx // 2 % nz
+def join_columns(packed, nz):
+    ny, nx = packed.shape
+    packed = jnp.concatenate(
+        join_rows([packed[e : e + PTS] for e in range(0, ny, PTS)], iota((PTS, nx), 0)), axis=0
+    )
+    plane = column_slot(iota((ny, nx), 1), nx) % nz
     up = (plane % PTS == PTS - 1) & (plane < nz - 1)
     down = (plane % PTS == 0) & (plane > 0)
     return (
@@ -276,24 +330,81 @@
     )
 
 
-def plane_kernel(u_ref, zp_ref):
-    fields, nz, ny, nx = u_ref.shape
+def along_y(left, pair, high_ref, low_ref):
+    _, _, ny, nx = high_ref.shape
+    rows = PTS * ny
+
+    def wide(ref):
+        return jnp.concatenate(
+            [ref[c, layer * PTS : (layer + 1) * PTS].reshape(rows, nx) for layer, c in pair],
+            axis=1,
+        )
+
+    high, low = wide(high_ref), wide(low_ref)
+    out = dot(left, jnp.concatenate([high, high, low], axis=0))
+    return [out[:, n * nx : (n + 1) * nx].reshape(PTS, ny, nx) for n in range(len(pair))]
+
+
+def along_x(right, layer, c, high_ref, low_ref):
+    _, _, ny, nx = high_ref.shape
+    zs = slice(layer * PTS, (layer + 1) * PTS)
+    high = high_ref[c, zs].reshape(PTS * ny, nx)
+    low = low_ref[c, zs].reshape(PTS * ny, nx)
+    out = dot(jnp.concatenate([high, low], axis=1), right)
+    return (out[:, 0:nx] + out[:, nx : 2 * nx]).reshape(PTS, ny, nx)
+
+
+def plane_kernel(table, f_ref, m_ref, right_ref, zp_ref):
+    _, comps, nz, ny, nx = f_ref.shape
     z_even = lax.axis_index("gz") % 2 == 0
-    for f in range(fields):
-        zp_ref[f] = assemble_plane(jnp.where(z_even, u_ref[f, nz - 1], u_ref[f, 0]), ny, nx)
-
-
-def assemble_kernel(u_ref, w_ref):
-    fields, nz, ny, nx = u_ref.shape
-    for f in range(fields):
+    at = jnp.where(z_even, nz - 1, 0)
+    z0 = jnp.where(z_even, nz - PTS, 0)
+    weights = [
+        jnp.where(z_even, float(table[w, PTS - 1]), float(table[w, 0])) for w in range(PTS)
+    ]
+    columns = row_columns(table.T, nx)
+    tall = jnp.concatenate([f_ref[0, c, at] for c in range(comps)], axis=0)
+    div_r = by_thrice(tall, right_ref[1])
+    for c in range(comps):
+        flux_s = f_ref[1, c, at]
+        div_s = [across_rows(flux_s[e : e + PTS], columns) for e in range(0, ny, PTS)]
+        div_t = joined([weights[w] * f_ref[2, c, z0 + w] for w in range(PTS)])
+        total = div_r[c * ny : (c + 1) * ny] + jnp.concatenate(div_s, axis=0) + div_t
+        zp_ref[c] = assemble_plane(total, ny, nx)
+    zp_ref[comps] = assemble_plane(m_ref[at].astype(F32), ny, nx)
+
+
+def diverge_kernel(table, f_ref, m_ref, left_ref, right_ref, w_ref, high_ref, low_ref, y_ref, x_ref):
+    _, comps, nz, ny, nx = f_ref.shape
+    blocks = [(layer, c) for layer in range(nz // PTS) for c in range(comps)]
+    for c in range(comps):
         for z in range(nz):
-            t = u_ref[f, z]
-            if z % PTS == PTS - 1 and z < nz - 1:
-                t = t + u_ref[f, z + 1]
+            high_ref[0, c, z], low_ref[0, c, z] = split(f_ref[0, c, z])
+            high_ref[1, c, z], low_ref[1, c, z] = split(f_ref[1, c, z])
+    for i in range(0, len(blocks), 2):
+        pair = blocks[i : i + 2]
+        sums = along_y(left_ref[1], pair, high_ref.at[1], low_ref.at[1])
+        for (layer, c), out in zip(pair, sums):
+            y_ref[c, layer * PTS : (layer + 1) * PTS] = out
+    for layer, c in blocks:
+        x_ref[c, layer * PTS : (layer + 1) * PTS] = along_x(
+            right_ref[1], layer, c, high_ref.at[0], low_ref.at[0]
+        )
+    for layer, c in blocks:
+        for e in range(0, ny, PTS):
+            ys = slice(e, e + PTS)
+            z0 = layer * PTS
+            out = combine_planes([f_ref[2, c, z0 + z, ys] for z in range(PTS)], table.T)
+            for z in range(PTS):
+                y_ref[c, z0 + z, ys] = out[z] + y_ref[c, z0 + z, ys] + x_ref[c, z0 + z, ys]
+    for f in range(comps + 1):
+        for z in range(nz):
             if z % PTS == 0 and z > 0:
                 w_ref[f, z] = w_ref[f, z - 1]
-            else:
-                w_ref[f, z] = assemble_plane(t, ny, nx)
+                continue
+            at = [z, z + 1] if z % PTS == PTS - 1 and z < nz - 1 else [z]
+            t = [m_ref[i].astype(F32) if f == comps else y_ref[f, i] for i in at]
+            w_ref[f, z] = assemble_plane(joined(t), ny, nx)
 
 
 def merge_sides(right, left):
@@ -473,7 +584,9 @@
 def call(kernel, outs, ins, scratch=(), out_specs=None, in_specs=None, flops=1 << 20):
     return pl.pallas_call(
         kernel,
-        out_shape=[jax.ShapeDtypeStruct(shape, F32) for shape in outs],
+        out_shape=[
+            out if hasattr(out, "dtype") else jax.ShapeDtypeStruct(out, F32) for out in outs
+        ],
         in_specs=in_specs or [VMEM] * len(ins),
         out_specs=out_specs or [VMEM] * len(outs),
         scratch_shapes=list(scratch),
@@ -482,32 +595,48 @@
     )(*ins)
 
 
-def local_part(velocity, geometry, mass_weights):
-    comps, nz, ny, nx = velocity.shape
+def local_part(table, velocity, geometry, mass_weights):
+    _, nz, ny, nx = velocity.shape
+    rows = PTS * ny
+    vector = (3, *velocity.shape)
     return call(
-        functools.partial(local_kernel, gll_derivative(ORDER)),
-        [(comps + 1, nz, ny, nx), (ny + SCALAR_ROWS, nx), velocity.shape],
+        functools.partial(local_kernel, table),
+        [
+            vector,
+            (ny + SCALAR_ROWS, nx),
+            velocity.shape,
+            jax.ShapeDtypeStruct(mass_weights.shape, BF16),
+            jax.ShapeDtypeStruct((2, rows, 3 * rows), BF16),
+            jax.ShapeDtypeStruct((4, 2 * nx, 2 * nx), BF16),
+        ],
         [
             pltpu.with_memory_space_constraint(x, pltpu.HBM)
             for x in (velocity, geometry, mass_weights)
         ],
         in_specs=[HBM] * 3,
         scratch=[
-            pltpu.VMEM(mass_weights.shape, BF16),
             pltpu.VMEM(geometry.shape, BF16),
-            pltpu.VMEM((3, *velocity.shape), F32),
-            pltpu.VMEM((3, *velocity.shape), BF16),
-            pltpu.VMEM((3, *velocity.shape), BF16),
-            pltpu.VMEM(velocity.shape, F32),
-            pltpu.VMEM((2, PTS * ny, 3 * PTS * ny), BF16),
-            pltpu.VMEM((2, 2 * nx, 2 * nx), BF16),
+            pltpu.VMEM(vector, F32),
+            pltpu.VMEM(velocity.shape, BF16),
+            pltpu.VMEM(velocity.shape, BF16),
             pltpu.SemaphoreType.DMA((nz // PTS, 3)),
         ],
     )
 
 
-def assembled(u):
-    return call(assemble_kernel, [u.shape], [u])[0]
+def diverged(table, fluxes, mass, left, right):
+    _, comps, nz, ny, nx = fluxes.shape
+    return call(
+        functools.partial(diverge_kernel, table),
+        [(comps + 1, nz, ny, nx)],
+        [fluxes, mass, left, right],
+        scratch=[
+            pltpu.VMEM((2, comps, nz, ny, nx), BF16),
+            pltpu.VMEM((2, comps, nz, ny, nx), BF16),
+            pltpu.VMEM((comps, nz, ny, nx), F32),
+            pltpu.VMEM((comps, nz, ny, nx), F32),
+        ],
+    )[0]
 
 
 def pairs_near(count):
@@ -521,9 +650,10 @@
 def few_rounds(sizes, velocity, geometry, mass_weights):
     comps, nz, ny, nx = velocity.shape
     fields = comps + 1
-    raw, px, held = local_part(velocity, geometry, mass_weights)
+    table = gll_derivative(ORDER)
+    fluxes, px, held, mass, left, right = local_part(table, velocity, geometry, mass_weights)
     qa = lax.ppermute(px, "gx", pairs_near(sizes[0]))
-    zp = call(plane_kernel, [(fields, ny, nx)], [raw])[0]
+    zp = call(functools.partial(plane_kernel, table), [(fields, ny, nx)], [fluxes, mass, right])[0]
     pb, pz, pd = call(
         first_kernel,
         [
@@ -542,7 +672,7 @@
         for k in range(sizes[2])
     ]
     qd = lax.ppermute(pd, ("gx", "gz"), both)
-    u = assembled(raw)
+    u = diverged(table, fluxes, mass, left, right)
     count = fields * nz
     pya, pyb, ps = call(
         second_kernel,
@@ -550,9 +680,14 @@
         [u, pb, qa, qb, qz, qd],
         scratch=[pltpu.VMEM((count, nx), F32)] * 2,
     )
+    apart = [
+        (i * sizes[1] + j, (i ^ 1) * sizes[1] + (j ^ 2))
+        for i in range(sizes[0])
+        for j in range(sizes[1])
+    ]
     qya = lax.ppermute(pya, "gy", pairs_near(sizes[1]))
     qyb = lax.ppermute(pyb, "gy", pairs_mirror(sizes[1]))
-    qs = lax.ppermute(ps, "gy", [(i, i ^ 2) for i in range(sizes[1])])
+    qs = lax.ppermute(ps, ("gx", "gy"), apart)
     w, mv = call(correct_kernel, [u.shape, velocity.shape], [held, u, qa, qb, qz, qd])
     residual, kinetic, enstrophy = call(
         functools.partial(last_kernel, sizes),
@@ -584,8 +719,9 @@
 
 def any_mesh(sizes, velocity, geometry, mass_weights):
     comps, nz, ny, nx = velocity.shape
-    raw, px, _ = local_part(velocity, geometry, mass_weights)
-    u = assembled(raw)
+    table = gll_derivative(ORDER)
+    fluxes, px, _, mass, left, right = local_part(table, velocity, geometry, mass_weights)
+    u = diverged(table, fluxes, mass, left, right)
     kinetic = 0.5 * jnp.sum(px[ny])
     enstrophy = jnp.sum(px[ny + 1])
     kinetic, enstrophy = lax.psum((kinetic, enstrophy), ("gx", "gy", "gz"))

time: 24.1 us -> 22.9 us (0.950)
  waiting for transfers between devices: 7.81 us -> 6.38 us
    ppermute x1, waiting for transfers between devices: 3.12 us -> 2.35 us  [few_rounds(): qd = lax.ppermute(pd, ('gx', 'gz'), both)]
    ppermute x1, waiting for transfers between devices: 3.96 us -> 3.43 us  [few_rounds(): qs = lax.ppermute(ps, ('gx', 'gy'), apart)]
  transfers between devices with their start and end apart: 7 -> 7, of which waited for: 3 -> 3; matrix products, arithmetic and copies ran while one was open for 0% -> 0% of each run, Pallas kernels for 5% -> 9%
where the time goes in v1:
time: 22.9 us; the launch traced here: 22.7 us
  starting transfers between devices  8.92 us (39%)
  Pallas kernels  6.76 us (30%)
  waiting for transfers between devices  6.38 us (28%)
  between operations  0.67 us (3%)
    pallas_call x7, Pallas kernels, call(): pl.pallas_call(kernel, out_shape=[out if hasattr(out, 'dtype') else jax.S...  6.76 us
    ppermute x1, waiting for transfers between devices, few_rounds(): qs = lax.ppermute(ps, ('gx', 'gy'), apart)  3.43 us
    ppermute x1, starting transfers between devices, few_rounds(): qz = lax.ppermute(pz, 'gz', pairs_near(sizes[2]))  2.91 us
    ppermute x1, starting transfers between devices, few_rounds(): qyb = lax.ppermute(pyb, 'gy', pairs_mirror(sizes[1]))  2.47 us
    ppermute x1, waiting for transfers between devices, few_rounds(): qd = lax.ppermute(pd, ('gx', 'gz'), both)  2.35 us
    ppermute x1, starting transfers between devices, few_rounds(): qya = lax.ppermute(pya, 'gy', pairs_near(sizes[1]))  1.64 us
    ppermute x1, starting transfers between devices, few_rounds(): qb = lax.ppermute(pb, 'gx', mirror)  0.98 us
    ppermute x1, waiting for transfers between devices, few_rounds(): qa = lax.ppermute(px, 'gx', pairs_near(sizes[0]))  0.59 us
  transfers between devices with their start and end apart: 7, of which 3 were waited for; matrix products, arithmetic and copies ran while one was open for 0% of the time, Pallas kernels for 9%

profile of v1, /device:TPU:0, one launch (start us, length us, event | category | flops | bytes accessed | tf_op | source)
XLA Modules:
  0.0 22.7 jit_solution(17181299488707742494)
XLA Ops:
  0.6 3.1 %shard_map.58 = (f32[3,3,16,32,128]{4,3,2,1,0:T(8,128)S(1)}, f32[40,128]{1,0:T(8,128)S(1)}, f32[3,16,32,128]{3,2,1,0:T(8,128)S(1)}, bf16[16,32,128]{2,1,0:T(8,12...) custom-call(f32[3,16,32,128]{3,2,1,0:T(8,128)} %v_hbm.1, bf16[6,16,32,128]{3,2,1,0:T(8,128)(2,1)} %g_hbm.1, ...), custom_call_target="tpu_custom_call" | custom-call | flops 1048576 | bytes 1048576 | tf_op jit(solution)/shard_map/pallas_call | solution.py:585
  3.8 0.6 %collective-permute-start = (f32[40,128]{1,0:T(8,128)S(1)}, f32[40,128]{1,0:T(8,128)S(1)}, u32[]{:S(2)}, u32[]{:S(2)}) collective-permute-start(f32[40,128]{1,0:T(8,128)S(1)} %get-tuple-element.25.px_ref), channel_id=1, source_target_pairs={{0,8},{8,0},{16,24},{24,16},{1,9},{9,1},{17,25},{25,17},{2,10},{10... | collective-permute-start | bytes 61448 | tf_op jit(solution)/shard_map/ppermute | solution.py:655
  4.3 0.2 %shard_map.60.zp_ref = f32[4,32,128]{2,1,0:T(8,128)S(1)} custom-call(f32[3,3,16,32,128]{4,3,2,1,0:T(8,128)S(1)} %get-tuple-element.21.f_ref, bf16[16,32,128]{2,1,0:T(8,128)(2,1)S(1)} %get-tuple-element.22.m_ref, bf16[4,256,256]{2,1,0:T(8,128)(2,1)S(1)} %get-tuple-element.24.right_ref), custom_call_target="tpu_custom_call" | custom-call | flops 1048576 | bytes 1048576 | tf_op jit(solution)/shard_map/pallas_call | solution.py:585
  4.6 0.6 %collective-permute-done.qa_ref = f32[40,128]{1,0:T(8,128)S(1)} collective-permute-done((f32[40,128]{1,0:T(8,128)S(1)}, f32[40,128]{1,0:T(8,128)S(1)}, u32[]{:S(2)}, u32[]{:S(2)}) %collective-permute-start) | collective-permute-done | bytes 20512 | tf_op jit(solution)/shard_map/ppermute | solution.py:655
  5.2 0.2 %shard_map.61 = (f32[40,128]{1,0:T(8,128)S(1)}, f32[136,128]{1,0:T(8,128)S(1)}, f32[16,128]{1,0:T(8,128)S(1)}) custom-call(f32[4,32,128]{2,1,0:T(8,128)S(1)} %shard_map.60.zp_ref, f32[40,128]{1,0:T(8,128)S(1)} %get-tuple-element.25.px_ref, f32[40,128]{1,0:T(8,128)S(1)} %collective-permute-done.qa_ref), custom_call_target="tpu_custom_call" | custom-call | flops 1048576 | bytes 1048576 | tf_op jit(solution)/shard_map/pallas_call | solution.py:585
  5.4 2.9 %collective-permute-start.2 = (f32[136,128]{1,0:T(8,128)S(1)}, f32[136,128]{1,0:T(8,128)S(1)}, u32[]{:S(2)}, u32[]{:S(2)}) collective-permute-start(f32[136,128]{1,0:T(8,128)S(1)} %get-tuple-element.27), channel_id=1, source_target_pairs={{0,1},{1,0},{2,3},{3,2},{4,5},{5,4},{6,7},{7,6},{8,9},{9,8},{10,11... | collective-permute-start | bytes 208904 | tf_op jit(solution)/shard_map/ppermute | solution.py:668
  8.3 1.0 %collective-permute-start.1 = (f32[40,128]{1,0:T(8,128)S(1)}, f32[40,128]{1,0:T(8,128)S(1)}, u32[]{:S(2)}, u32[]{:S(2)}) collective-permute-start(f32[40,128]{1,0:T(8,128)S(1)} %get-tuple-element.26.pb_ref), channel_id=1, source_target_pairs={{0,24},{8,16},{16,8},{24,0},{1,25},{9,17},{17,9},{25,1},{2,26},{10... | collective-permute-start | bytes 61448 | tf_op jit(solution)/shard_map/ppermute | solution.py:667
  9.3 0.3 %collective-permute-start.3 = (f32[16,128]{1,0:T(8,128)S(1)}, f32[16,128]{1,0:T(8,128)S(1)}, u32[]{:S(2)}, u32[]{:S(2)}) collective-permute-start(f32[16,128]{1,0:T(8,128)S(1)} %get-tuple-element.28), channel_id=1, source_target_pairs={{0,25},{1,24},{8,17},{9,16},{16,9},{17,8},{24,1},{25,0},{2,27},{3,... | collective-permute-start | bytes 24584 | tf_op jit(solution)/shard_map/ppermute | solution.py:674
  9.6 1.3 %shard_map.59.u_ref = f32[4,16,32,128]{3,2,1,0:T(8,128)S(1)} custom-call(f32[3,3,16,32,128]{4,3,2,1,0:T(8,128)S(1)} %get-tuple-element.21.f_ref, bf16[16,32,128]{2,1,0:T(8,128)(2,1)S(1)} %get-tuple-element.22.m_ref, bf16[2,256,768]{2,1,0:T(8,128)(2,1)S(1)} %get-tuple-element.23.left_ref, bf16[4,256,256]{2,1,0:T(8,128)(2,1)S(1)} %get-tuple-element.24.right_ref), custom_call_target="tpu_custom_call" | custom-call | flops 1048576 | bytes 1048576 | tf_op jit(solution)/shard_map/pallas_call | solution.py:585
  10.9 2.3 %collective-permute-done.3.qd_ref = f32[16,128]{1,0:T(8,128)S(1)} collective-permute-done((f32[16,128]{1,0:T(8,128)S(1)}, f32[16,128]{1,0:T(8,128)S(1)}, u32[]{:S(2)}, u32[]{:S(2)}) %collective-permute-start.3) | collective-permute-done | bytes 8224 | tf_op jit(solution)/shard_map/ppermute | solution.py:674
  13.3 0.0 collective-permute-done.1.qb_ref
  13.3 0.0 collective-permute-done.2.qz_ref
  13.3 0.3 %shard_map.63 = (f32[72,128]{1,0:T(8,128)S(1)}, f32[72,128]{1,0:T(8,128)S(1)}, f32[8,128]{1,0:T(8,128)S(1)}) custom-call(f32[4,16,32,128]{3,2,1,0:T(8,128)S(1)} %shard_map.59.u_ref, f32[40,128]{1,0:T(8,128)S(1)} %get-tuple-element.26.pb_ref, f32[40,128]{1,0:T(8,128)S(1)} %collective-permute-done.qa_ref, f32[40,128]{1,0:T(8,128)S(1)} %collective-permute-done.1.qb_ref, ...), custom_call_target="tpu_custom_call" | custom-call | flops 1048576 | bytes 1048576 | tf_op jit(solution)/shard_map/pallas_call | solution.py:585
  13.6 1.6 %collective-permute-start.4 = (f32[72,128]{1,0:T(8,128)S(1)}, f32[72,128]{1,0:T(8,128)S(1)}, u32[]{:S(2)}, u32[]{:S(2)}) collective-permute-start(f32[72,128]{1,0:T(8,128)S(1)} %get-tuple-element.31), channel_id=1, source_target_pairs={{0,2},{2,0},{4,6},{6,4},{1,3},{3,1},{5,7},{7,5},{8,10},{10,8},{12,... | collective-permute-start | bytes 110600 | tf_op jit(solution)/shard_map/ppermute | solution.py:688
  15.2 2.5 %collective-permute-start.5 = (f32[72,128]{1,0:T(8,128)S(1)}, f32[72,128]{1,0:T(8,128)S(1)}, u32[]{:S(2)}, u32[]{:S(2)}) collective-permute-start(f32[72,128]{1,0:T(8,128)S(1)} %get-tuple-element.32), channel_id=1, source_target_pairs={{0,6},{2,4},{4,2},{6,0},{1,7},{3,5},{5,3},{7,1},{8,14},{10,12},{12... | collective-permute-start | bytes 110600 | tf_op jit(solution)/shard_map/ppermute | solution.py:689
  17.7 0.1 collective-permute-start.6
  17.8 0.4 %shard_map.62 = (f32[4,16,32,128]{3,2,1,0:T(8,128)S(1)}, f32[3,16,32,128]{3,2,1,0:T(8,128)S(1)}) custom-call(f32[3,16,32,128]{3,2,1,0:T(8,128)S(1)} %get-tuple-element.20.v_ref, f32[4,16,32,128]{3,2,1,0:T(8,128)S(1)} %shard_map.59.u_ref, f32[40,128]{1,0:T(8,128)S(1)} %collective-permute-done.qa_ref, f32[40,128]{1,0:T(8,128)S(1)} %collective-permute-done.1.qb_ref, ...), custom_call_target="tpu_custom_call" | custom-call | flops 1048576 | bytes 1048576 | tf_op jit(solution)/shard_map/pallas_call | solution.py:585
  18.2 3.4 %collective-permute-done.6.qs_ref = f32[8,128]{1,0:T(8,128)S(1)} collective-permute-done((f32[8,128]{1,0:T(8,128)S(1)}, f32[8,128]{1,0:T(8,128)S(1)}, u32[]{:S(2)}, u32[]{:S(2)}) %collective-permute-start.6) | collective-permute-done | bytes 4128 | tf_op jit(solution)/shard_map/ppermute | solution.py:690
  21.6 0.0 collective-permute-done.4.qya_ref
  21.6 0.0 collective-permute-done.5.qyb_ref
  21.6 1.1 %shard_map.64 = (f32[3,16,32,128]{3,2,1,0:T(8,128)}, f32[1,1]{1,0:T(1,128)}, f32[1,1]{1,0:T(1,128)}) custom-call(f32[3,16,32,128]{3,2,1,0:T(8,128)S(1)} %get-tuple-element.20.v_ref, f32[4,16,32,128]{3,2,1,0:T(8,128)S(1)} %get-tuple-element.29.w_ref, f32[3,16,32,128]{3,2,1,0:T(8,128)S(1)} %get-tuple-element.30.mv_ref, ...), custom_call_target="tpu_custom_call" | custom-call | flops 1048576 | bytes 1048576 | tf_op jit(solution)/shard_map/pallas_call | solution.py:585
Async XLA Ops:
  3.8 1.4 %collective-permute-start = (f32[40,128]{1,0:T(8,128)S(1)}, f32[40,128]{1,0:T(8,128)S(1)}, u32[]{:S(2)}, u32[]{:S(2)}) collective-permute-start(f32[40,128]{1,0:T(8,128)S(1)} %get-tuple-element.25.px_ref), channel_id=1, source_target_pairs={{0,8},{8,0},{16,24},{24,16},{1,9},{9,1},{17,25},{25,17},{2,10},{10... | collective-permute-start | bytes 61448 | tf_op jit(solution)/shard_map/ppermute | solution.py:655
  5.4 7.9 %collective-permute-start.2 = (f32[136,128]{1,0:T(8,128)S(1)}, f32[136,128]{1,0:T(8,128)S(1)}, u32[]{:S(2)}, u32[]{:S(2)}) collective-permute-start(f32[136,128]{1,0:T(8,128)S(1)} %get-tuple-element.27), channel_id=1, source_target_pairs={{0,1},{1,0},{2,3},{3,2},{4,5},{5,4},{6,7},{7,6},{8,9},{9,8},{10,11... | collective-permute-start | bytes 208904 | tf_op jit(solution)/shard_map/ppermute | solution.py:668
  8.3 5.0 %collective-permute-start.1 = (f32[40,128]{1,0:T(8,128)S(1)}, f32[40,128]{1,0:T(8,128)S(1)}, u32[]{:S(2)}, u32[]{:S(2)}) collective-permute-start(f32[40,128]{1,0:T(8,128)S(1)} %get-tuple-element.26.pb_ref), channel_id=1, source_target_pairs={{0,24},{8,16},{16,8},{24,0},{1,25},{9,17},{17,9},{25,1},{2,26},{10... | collective-permute-start | bytes 61448 | tf_op jit(solution)/shard_map/ppermute | solution.py:667
  9.3 4.0 %collective-permute-start.3 = (f32[16,128]{1,0:T(8,128)S(1)}, f32[16,128]{1,0:T(8,128)S(1)}, u32[]{:S(2)}, u32[]{:S(2)}) collective-permute-start(f32[16,128]{1,0:T(8,128)S(1)} %get-tuple-element.28), channel_id=1, source_target_pairs={{0,25},{1,24},{8,17},{9,16},{16,9},{17,8},{24,1},{25,0},{2,27},{3,... | collective-permute-start | bytes 24584 | tf_op jit(solution)/shard_map/ppermute | solution.py:674
  13.6 8.1 %collective-permute-start.4 = (f32[72,128]{1,0:T(8,128)S(1)}, f32[72,128]{1,0:T(8,128)S(1)}, u32[]{:S(2)}, u32[]{:S(2)}) collective-permute-start(f32[72,128]{1,0:T(8,128)S(1)} %get-tuple-element.31), channel_id=1, source_target_pairs={{0,2},{2,0},{4,6},{6,4},{1,3},{3,1},{5,7},{7,5},{8,10},{10,8},{12,... | collective-permute-start | bytes 110600 | tf_op jit(solution)/shard_map/ppermute | solution.py:688
  15.2 6.4 %collective-permute-start.5 = (f32[72,128]{1,0:T(8,128)S(1)}, f32[72,128]{1,0:T(8,128)S(1)}, u32[]{:S(2)}, u32[]{:S(2)}) collective-permute-start(f32[72,128]{1,0:T(8,128)S(1)} %get-tuple-element.32), channel_id=1, source_target_pairs={{0,6},{2,4},{4,2},{6,0},{1,7},{3,5},{5,3},{7,1},{8,14},{10,12},{12... | collective-permute-start | bytes 110600 | tf_op jit(solution)/shard_map/ppermute | solution.py:689
  17.7 3.9 %collective-permute-start.6 = (f32[8,128]{1,0:T(8,128)S(1)}, f32[8,128]{1,0:T(8,128)S(1)}, u32[]{:S(2)}, u32[]{:S(2)}) collective-permute-start(f32[8,128]{1,0:T(8,128)S(1)} %get-tuple-element.33.ps_ref), channel_id=1, source_target_pairs={{0,12},{2,14},{4,8},{6,10},{8,4},{10,6},{12,0},{14,2},{16,28},{18,... | collective-permute-start | bytes 12296 | tf_op jit(solution)/shard_map/ppermute | solution.py:690

commit v2 on v1

--- a/solution.py
+++ b/solution.py
@@ -374,7 +374,9 @@
     zp_ref[comps] = assemble_plane(m_ref[at].astype(F32), ny, nx)
 
 
-def diverge_kernel(table, f_ref, m_ref, left_ref, right_ref, w_ref, high_ref, low_ref, y_ref, x_ref):
+def diverge_kernel(
+    table, f_ref, m_ref, left_ref, right_ref, w_ref, ends_ref, high_ref, low_ref, y_ref, x_ref
+):
     _, comps, nz, ny, nx = f_ref.shape
     blocks = [(layer, c) for layer in range(nz // PTS) for c in range(comps)]
     for c in range(comps):
@@ -399,12 +401,17 @@
                 y_ref[c, z0 + z, ys] = out[z] + y_ref[c, z0 + z, ys] + x_ref[c, z0 + z, ys]
     for f in range(comps + 1):
         for z in range(nz):
+            j = ends_ref.shape[1] - 1 - f * nz - z
             if z % PTS == 0 and z > 0:
                 w_ref[f, z] = w_ref[f, z - 1]
+                ends_ref[:, j] = ends_ref[:, j + 1]
                 continue
             at = [z, z + 1] if z % PTS == PTS - 1 and z < nz - 1 else [z]
             t = [m_ref[i].astype(F32) if f == comps else y_ref[f, i] for i in at]
-            w_ref[f, z] = assemble_plane(joined(t), ny, nx)
+            whole = assemble_plane(joined(t), ny, nx)
+            w_ref[f, z] = whole
+            ends_ref[0, j : j + 1] = whole[0:1]
+            ends_ref[1, j : j + 1] = whole[ny - 1 : ny]
 
 
 def merge_sides(right, left):
@@ -453,28 +460,34 @@
     return merge_sides(jnp.where(x_even, 0.0, qd), jnp.where(x_even, qd, 0.0))
 
 
+def spread_columns(merged, count):
+    nx = merged.shape[1]
+    rows = jnp.broadcast_to(merged, (count, nx))
+    rows = pltpu.roll(rows, (nx + 1 - 2 * count) % nx, 1, stride=2, stride_axis=0)
+    lane = iota((count, nx), 1)
+    return jnp.where((lane == 0) | (lane == nx - 1), rows, 0.0)
+
+
 def second_kernel(
-    u_ref, pb_ref, qa_ref, qb_ref, qz_ref, qd_ref, pya_ref, pyb_ref, ps_ref, low_ref, high_ref
+    ends_ref, pb_ref, qa_ref, qb_ref, qz_ref, qd_ref, pya_ref, pyb_ref, ps_ref, low_ref, high_ref
 ):
-    fields, nz, ny, nx = u_ref.shape
+    _, count, nx = ends_ref.shape
+    ny = pb_ref.shape[0] - SCALAR_ROWS
+    fields = (qz_ref.shape[0] - SCALAR_ROWS) // ny
+    nz = count // fields
     x_even = lax.axis_index("gx") % 2 == 0
     y_even = lax.axis_index("gy") % 2 == 0
-    for ys, row, out in (
-        (slice(0, PTS), 0, low_ref),
-        (slice(ny - PTS, ny), PTS - 1, high_ref),
-    ):
-        merged = x_sides(qa_ref[ys], qb_ref[ys], x_even)
-        diag = diagonal_sides(qd_ref[0:PTS], x_even)
+    diag = diagonal_sides(qd_ref[0:PTS], x_even)
+    for i, (y, out) in enumerate(((0, low_ref), (ny - 1, high_ref))):
+        merged = x_sides(qa_ref[y : y + 1], qb_ref[y : y + 1], x_even)
+        out[...] = ends_ref[i] + spread_columns(merged, count)
         for f in range(fields):
-            for z in range(nz):
-                j = f * nz + z
-                t = u_ref[f, z, ys] + place_columns(merged, j, nx)
-                if z in (0, nz - 1):
-                    t = t + qz_ref[f * ny + ys.start : f * ny + ys.stop]
-                    t = t + place_columns(diag, f * nz + ys.start // PTS, nx)
-                out[j : j + 1] = t[row : row + 1]
+            corner = place_columns(diag, f * nz + y // PTS, nx)[y % PTS : y % PTS + 1]
+            extra = qz_ref[f * ny + y : f * ny + y + 1] + corner
+            for z in (0, nz - 1):
+                j = count - 1 - f * nz - z
+                out[j : j + 1] = out[j : j + 1] + extra
     sums = pb_ref[ny:] + qb_ref[ny:] + qz_ref[fields * ny :] + qd_ref[PTS:]
-    count = fields * nz
     pya_ref[0:count] = jnp.where(y_even, high_ref[...], low_ref[...])
     pyb_ref[0:count] = jnp.where(y_even, low_ref[...], high_ref[...])
     pya_ref[count:] = sums
@@ -556,12 +569,12 @@
             edge = e == 0 or e == ny - PTS
             side, at = (low_ref, 0) if e == 0 else (high_ref, PTS - 1)
             if edge:
-                j = (fields - 1) * nz + z
+                j = nz - 1 - z
                 extra = rayleigh * jnp.where(sub == at, side[j : j + 1], 0.0)
             for c in range(fields - 1):
                 t = w_ref[c, z, ys] - rayleigh * mv_ref[c, z, ys]
                 if edge:
-                    j = c * nz + z
+                    j = count - 1 - c * nz - z
                     t = t + jnp.where(sub == at, side[j : j + 1], 0.0)
                     t = t - extra * v_ref[c, z, ys]
                 out_ref[c, z, ys] = jnp.where(keep[ys], t, 0.0)
@@ -628,7 +641,7 @@
     _, comps, nz, ny, nx = fluxes.shape
     return call(
         functools.partial(diverge_kernel, table),
-        [(comps + 1, nz, ny, nx)],
+        [(comps + 1, nz, ny, nx), (2, (comps + 1) * nz, nx)],
         [fluxes, mass, left, right],
         scratch=[
             pltpu.VMEM((2, comps, nz, ny, nx), BF16),
@@ -636,7 +649,7 @@
             pltpu.VMEM((comps, nz, ny, nx), F32),
             pltpu.VMEM((comps, nz, ny, nx), F32),
         ],
-    )[0]
+    )
 
 
 def pairs_near(count):
@@ -672,12 +685,12 @@
         for k in range(sizes[2])
     ]
     qd = lax.ppermute(pd, ("gx", "gz"), both)
-    u = diverged(table, fluxes, mass, left, right)
+    u, ends = diverged(table, fluxes, mass, left, right)
     count = fields * nz
     pya, pyb, ps = call(
         second_kernel,
         [(count + SCALAR_ROWS, nx), (count + SCALAR_ROWS, nx), (SCALAR_ROWS, nx)],
-        [u, pb, qa, qb, qz, qd],
+        [ends, pb, qa, qb, qz, qd],
         scratch=[pltpu.VMEM((count, nx), F32)] * 2,
     )
     apart = [
@@ -721,7 +734,7 @@
     comps, nz, ny, nx = velocity.shape
     table = gll_derivative(ORDER)
     fluxes, px, _, mass, left, right = local_part(table, velocity, geometry, mass_weights)
-    u = diverged(table, fluxes, mass, left, right)
+    u, _ = diverged(table, fluxes, mass, left, right)
     kinetic = 0.5 * jnp.sum(px[ny])
     enstrophy = jnp.sum(px[ny + 1])
     kinetic, enstrophy = lax.psum((kinetic, enstrophy), ("gx", "gy", "gz"))

time: 22.9 us -> 22.8 us (level)
  no operation moved by 1% of the time
where the time goes in v2:
time: 22.8 us; the launch traced here: 22.6 us
  starting transfers between devices  8.92 us (39%)
  Pallas kernels  6.65 us (29%)
  waiting for transfers between devices  6.37 us (28%)
  between operations  0.68 us (3%)
    pallas_call x7, Pallas kernels, call(): pl.pallas_call(kernel, out_shape=[out if hasattr(out, 'dtype') else jax.S...  6.65 us
    ppermute x1, waiting for transfers between devices, few_rounds(): qs = lax.ppermute(ps, ('gx', 'gy'), apart)  3.43 us
    ppermute x1, starting transfers between devices, few_rounds(): qz = lax.ppermute(pz, 'gz', pairs_near(sizes[2]))  2.91 us
    ppermute x1, starting transfers between devices, few_rounds(): qyb = lax.ppermute(pyb, 'gy', pairs_mirror(sizes[1]))  2.47 us
    ppermute x1, waiting for transfers between devices, few_rounds(): qd = lax.ppermute(pd, ('gx', 'gz'), both)  2.34 us
    ppermute x1, starting transfers between devices, few_rounds(): qya = lax.ppermute(pya, 'gy', pairs_near(sizes[1]))  1.64 us
    ppermute x1, starting transfers between devices, few_rounds(): qb = lax.ppermute(pb, 'gx', mirror)  0.98 us
    ppermute x1, waiting for transfers between devices, few_rounds(): qa = lax.ppermute(px, 'gx', pairs_near(sizes[0]))  0.59 us
  transfers between devices with their start and end apart: 7, of which 3 were waited for; matrix products, arithmetic and copies ran while one was open for 0% of the time, Pallas kernels for 9%

profile of v2, /device:TPU:0, one launch (start us, length us, event | category | flops | bytes accessed | tf_op | source)
XLA Modules:
  0.0 22.6 jit_solution(9461483323646056203)
XLA Ops:
  0.6 3.1 %shard_map.58 = (f32[3,3,16,32,128]{4,3,2,1,0:T(8,128)S(1)}, f32[40,128]{1,0:T(8,128)S(1)}, f32[3,16,32,128]{3,2,1,0:T(8,128)S(1)}, bf16[16,32,128]{2,1,0:T(8,12...) custom-call(f32[3,16,32,128]{3,2,1,0:T(8,128)} %v_hbm.1, bf16[6,16,32,128]{3,2,1,0:T(8,128)(2,1)} %g_hbm.1, ...), custom_call_target="tpu_custom_call" | custom-call | flops 1048576 | bytes 1048576 | tf_op jit(solution)/shard_map/pallas_call | solution.py:598
  3.8 0.6 %collective-permute-start = (f32[40,128]{1,0:T(8,128)S(1)}, f32[40,128]{1,0:T(8,128)S(1)}, u32[]{:S(2)}, u32[]{:S(2)}) collective-permute-start(f32[40,128]{1,0:T(8,128)S(1)} %get-tuple-element.28.px_ref), channel_id=1, source_target_pairs={{0,8},{8,0},{16,24},{24,16},{1,9},{9,1},{17,25},{25,17},{2,10},{10... | collective-permute-start | bytes 61448 | tf_op jit(solution)/shard_map/ppermute | solution.py:668
  4.3 0.2 %shard_map.60.zp_ref = f32[4,32,128]{2,1,0:T(8,128)S(1)} custom-call(f32[3,3,16,32,128]{4,3,2,1,0:T(8,128)S(1)} %get-tuple-element.23.f_ref, bf16[16,32,128]{2,1,0:T(8,128)(2,1)S(1)} %get-tuple-element.24.m_ref, bf16[4,256,256]{2,1,0:T(8,128)(2,1)S(1)} %get-tuple-element.26.right_ref), custom_call_target="tpu_custom_call" | custom-call | flops 1048576 | bytes 1048576 | tf_op jit(solution)/shard_map/pallas_call | solution.py:598
  4.6 0.6 %collective-permute-done.qa_ref = f32[40,128]{1,0:T(8,128)S(1)} collective-permute-done((f32[40,128]{1,0:T(8,128)S(1)}, f32[40,128]{1,0:T(8,128)S(1)}, u32[]{:S(2)}, u32[]{:S(2)}) %collective-permute-start) | collective-permute-done | bytes 20512 | tf_op jit(solution)/shard_map/ppermute | solution.py:668
  5.2 0.2 %shard_map.61 = (f32[40,128]{1,0:T(8,128)S(1)}, f32[136,128]{1,0:T(8,128)S(1)}, f32[16,128]{1,0:T(8,128)S(1)}) custom-call(f32[4,32,128]{2,1,0:T(8,128)S(1)} %shard_map.60.zp_ref, f32[40,128]{1,0:T(8,128)S(1)} %get-tuple-element.28.px_ref, f32[40,128]{1,0:T(8,128)S(1)} %collective-permute-done.qa_ref), custom_call_target="tpu_custom_call" | custom-call | flops 1048576 | bytes 1048576 | tf_op jit(solution)/shard_map/pallas_call | solution.py:598
  5.4 2.9 %collective-permute-start.2 = (f32[136,128]{1,0:T(8,128)S(1)}, f32[136,128]{1,0:T(8,128)S(1)}, u32[]{:S(2)}, u32[]{:S(2)}) collective-permute-start(f32[136,128]{1,0:T(8,128)S(1)} %get-tuple-element.30), channel_id=1, source_target_pairs={{0,1},{1,0},{2,3},{3,2},{4,5},{5,4},{6,7},{7,6},{8,9},{9,8},{10,11... | collective-permute-start | bytes 208904 | tf_op jit(solution)/shard_map/ppermute | solution.py:681
  8.3 1.0 %collective-permute-start.1 = (f32[40,128]{1,0:T(8,128)S(1)}, f32[40,128]{1,0:T(8,128)S(1)}, u32[]{:S(2)}, u32[]{:S(2)}) collective-permute-start(f32[40,128]{1,0:T(8,128)S(1)} %get-tuple-element.29.pb_ref), channel_id=1, source_target_pairs={{0,24},{8,16},{16,8},{24,0},{1,25},{9,17},{17,9},{25,1},{2,26},{10... | collective-permute-start | bytes 61448 | tf_op jit(solution)/shard_map/ppermute | solution.py:680
  9.3 0.3 %collective-permute-start.3 = (f32[16,128]{1,0:T(8,128)S(1)}, f32[16,128]{1,0:T(8,128)S(1)}, u32[]{:S(2)}, u32[]{:S(2)}) collective-permute-start(f32[16,128]{1,0:T(8,128)S(1)} %get-tuple-element.31), channel_id=1, source_target_pairs={{0,25},{1,24},{8,17},{9,16},{16,9},{17,8},{24,1},{25,0},{2,27},{3,... | collective-permute-start | bytes 24584 | tf_op jit(solution)/shard_map/ppermute | solution.py:687
  9.6 1.3 %shard_map.59 = (f32[4,16,32,128]{3,2,1,0:T(8,128)S(1)}, f32[2,64,128]{2,1,0:T(8,128)S(1)}) custom-call(f32[3,3,16,32,128]{4,3,2,1,0:T(8,128)S(1)} %get-tuple-element.23.f_ref, bf16[16,32,128]{2,1,0:T(8,128)(2,1)S(1)} %get-tuple-element.24.m_ref, bf16[2,256,768]{2,1,0:T(8,128)(2,1)S(1)} %get-tuple-element.25.left_ref, ...), custom_call_target="tpu_custom_call" | custom-call | flops 1048576 | bytes 1048576 | tf_op jit(solution)/shard_map/pallas_call | solution.py:598
  10.9 2.3 %collective-permute-done.3.qd_ref = f32[16,128]{1,0:T(8,128)S(1)} collective-permute-done((f32[16,128]{1,0:T(8,128)S(1)}, f32[16,128]{1,0:T(8,128)S(1)}, u32[]{:S(2)}, u32[]{:S(2)}) %collective-permute-start.3) | collective-permute-done | bytes 8224 | tf_op jit(solution)/shard_map/ppermute | solution.py:687
  13.3 0.0 collective-permute-done.1.qb_ref
  13.3 0.0 collective-permute-done.2.qz_ref
  13.3 0.2 shard_map.63
  13.5 1.6 %collective-permute-start.4 = (f32[72,128]{1,0:T(8,128)S(1)}, f32[72,128]{1,0:T(8,128)S(1)}, u32[]{:S(2)}, u32[]{:S(2)}) collective-permute-start(f32[72,128]{1,0:T(8,128)S(1)} %get-tuple-element.35), channel_id=1, source_target_pairs={{0,2},{2,0},{4,6},{6,4},{1,3},{3,1},{5,7},{7,5},{8,10},{10,8},{12,... | collective-permute-start | bytes 110600 | tf_op jit(solution)/shard_map/ppermute | solution.py:701
  15.1 2.5 %collective-permute-start.5 = (f32[72,128]{1,0:T(8,128)S(1)}, f32[72,128]{1,0:T(8,128)S(1)}, u32[]{:S(2)}, u32[]{:S(2)}) collective-permute-start(f32[72,128]{1,0:T(8,128)S(1)} %get-tuple-element.36), channel_id=1, source_target_pairs={{0,6},{2,4},{4,2},{6,0},{1,7},{3,5},{5,3},{7,1},{8,14},{10,12},{12... | collective-permute-start | bytes 110600 | tf_op jit(solution)/shard_map/ppermute | solution.py:702
  17.6 0.1 collective-permute-start.6
  17.7 0.4 %shard_map.62 = (f32[4,16,32,128]{3,2,1,0:T(8,128)S(1)}, f32[3,16,32,128]{3,2,1,0:T(8,128)S(1)}) custom-call(f32[3,16,32,128]{3,2,1,0:T(8,128)S(1)} %get-tuple-element.22.v_ref, f32[4,16,32,128]{3,2,1,0:T(8,128)S(1)} %get-tuple-element.27.u_ref, f32[40,128]{1,0:T(8,128)S(1)} %collective-permute-done.qa_ref, f32[40,128]{1,0:T(8,128)S(1)} %collective-permute-done.1.qb_ref, ...), custom_call_target="tpu_custom_call" | custom-call | flops 1048576 | bytes 1048576 | tf_op jit(solution)/shard_map/pallas_call | solution.py:598
  18.1 3.4 %collective-permute-done.6.qs_ref = f32[8,128]{1,0:T(8,128)S(1)} collective-permute-done((f32[8,128]{1,0:T(8,128)S(1)}, f32[8,128]{1,0:T(8,128)S(1)}, u32[]{:S(2)}, u32[]{:S(2)}) %collective-permute-start.6) | collective-permute-done | bytes 4128 | tf_op jit(solution)/shard_map/ppermute | solution.py:703
  21.5 0.0 collective-permute-done.4.qya_ref
  21.5 0.0 collective-permute-done.5.qyb_ref
  21.5 1.1 %shard_map.64 = (f32[3,16,32,128]{3,2,1,0:T(8,128)}, f32[1,1]{1,0:T(1,128)}, f32[1,1]{1,0:T(1,128)}) custom-call(f32[3,16,32,128]{3,2,1,0:T(8,128)S(1)} %get-tuple-element.22.v_ref, f32[4,16,32,128]{3,2,1,0:T(8,128)S(1)} %get-tuple-element.32.w_ref, f32[3,16,32,128]{3,2,1,0:T(8,128)S(1)} %get-tuple-element.33.mv_ref, ...), custom_call_target="tpu_custom_call" | custom-call | flops 1048576 | bytes 1048576 | tf_op jit(solution)/shard_map/pallas_call | solution.py:598
Async XLA Ops:
  3.8 1.4 %collective-permute-start = (f32[40,128]{1,0:T(8,128)S(1)}, f32[40,128]{1,0:T(8,128)S(1)}, u32[]{:S(2)}, u32[]{:S(2)}) collective-permute-start(f32[40,128]{1,0:T(8,128)S(1)} %get-tuple-element.28.px_ref), channel_id=1, source_target_pairs={{0,8},{8,0},{16,24},{24,16},{1,9},{9,1},{17,25},{25,17},{2,10},{10... | collective-permute-start | bytes 61448 | tf_op jit(solution)/shard_map/ppermute | solution.py:668
  5.4 7.9 %collective-permute-start.2 = (f32[136,128]{1,0:T(8,128)S(1)}, f32[136,128]{1,0:T(8,128)S(1)}, u32[]{:S(2)}, u32[]{:S(2)}) collective-permute-start(f32[136,128]{1,0:T(8,128)S(1)} %get-tuple-element.30), channel_id=1, source_target_pairs={{0,1},{1,0},{2,3},{3,2},{4,5},{5,4},{6,7},{7,6},{8,9},{9,8},{10,11... | collective-permute-start | bytes 208904 | tf_op jit(solution)/shard_map/ppermute | solution.py:681
  8.3 5.0 %collective-permute-start.1 = (f32[40,128]{1,0:T(8,128)S(1)}, f32[40,128]{1,0:T(8,128)S(1)}, u32[]{:S(2)}, u32[]{:S(2)}) collective-permute-start(f32[40,128]{1,0:T(8,128)S(1)} %get-tuple-element.29.pb_ref), channel_id=1, source_target_pairs={{0,24},{8,16},{16,8},{24,0},{1,25},{9,17},{17,9},{25,1},{2,26},{10... | collective-permute-start | bytes 61448 | tf_op jit(solution)/shard_map/ppermute | solution.py:680
  9.3 4.0 %collective-permute-start.3 = (f32[16,128]{1,0:T(8,128)S(1)}, f32[16,128]{1,0:T(8,128)S(1)}, u32[]{:S(2)}, u32[]{:S(2)}) collective-permute-start(f32[16,128]{1,0:T(8,128)S(1)} %get-tuple-element.31), channel_id=1, source_target_pairs={{0,25},{1,24},{8,17},{9,16},{16,9},{17,8},{24,1},{25,0},{2,27},{3,... | collective-permute-start | bytes 24584 | tf_op jit(solution)/shard_map/ppermute | solution.py:687
  13.5 8.1 %collective-permute-start.4 = (f32[72,128]{1,0:T(8,128)S(1)}, f32[72,128]{1,0:T(8,128)S(1)}, u32[]{:S(2)}, u32[]{:S(2)}) collective-permute-start(f32[72,128]{1,0:T(8,128)S(1)} %get-tuple-element.35), channel_id=1, source_target_pairs={{0,2},{2,0},{4,6},{6,4},{1,3},{3,1},{5,7},{7,5},{8,10},{10,8},{12,... | collective-permute-start | bytes 110600 | tf_op jit(solution)/shard_map/ppermute | solution.py:701
  15.1 6.4 %collective-permute-start.5 = (f32[72,128]{1,0:T(8,128)S(1)}, f32[72,128]{1,0:T(8,128)S(1)}, u32[]{:S(2)}, u32[]{:S(2)}) collective-permute-start(f32[72,128]{1,0:T(8,128)S(1)} %get-tuple-element.36), channel_id=1, source_target_pairs={{0,6},{2,4},{4,2},{6,0},{1,7},{3,5},{5,3},{7,1},{8,14},{10,12},{12... | collective-permute-start | bytes 110600 | tf_op jit(solution)/shard_map/ppermute | solution.py:702
  17.6 3.9 %collective-permute-start.6 = (f32[8,128]{1,0:T(8,128)S(1)}, f32[8,128]{1,0:T(8,128)S(1)}, u32[]{:S(2)}, u32[]{:S(2)}) collective-permute-start(f32[8,128]{1,0:T(8,128)S(1)} %get-tuple-element.37.ps_ref), channel_id=1, source_target_pairs={{0,12},{2,14},{4,8},{6,10},{8,4},{10,6},{12,0},{14,2},{16,28},{18,... | collective-permute-start | bytes 12296 | tf_op jit(solution)/shard_map/ppermute | solution.py:703

commit v3 on v2

--- a/solution.py
+++ b/solution.py
@@ -354,7 +354,7 @@
     return (out[:, 0:nx] + out[:, nx : 2 * nx]).reshape(PTS, ny, nx)
 
 
-def plane_kernel(table, f_ref, m_ref, right_ref, zp_ref):
+def plane_kernel(table, f_ref, m_ref, right_ref, px_ref, zp_ref, edge_ref):
     _, comps, nz, ny, nx = f_ref.shape
     z_even = lax.axis_index("gz") % 2 == 0
     at = jnp.where(z_even, nz - 1, 0)
@@ -372,6 +372,15 @@
         total = div_r[c * ny : (c + 1) * ny] + jnp.concatenate(div_s, axis=0) + div_t
         zp_ref[c] = assemble_plane(total, ny, nx)
     zp_ref[comps] = assemble_plane(m_ref[at].astype(F32), ny, nx)
+    lane = iota((PTS, nx), 1)
+    edge = None
+    for e in range(ny // PTS):
+        t = px_ref[e * PTS : (e + 1) * PTS]
+        t = jnp.where(z_even, pltpu.roll(t, nx - 2 * (nz - 1), 1), t)
+        t = pltpu.roll(t, 2 * e, 1) if e else t
+        mine = (lane + 1) % nx // 2 % nz == e
+        edge = jnp.where(mine, t, 0.0 if edge is None else edge)
+    edge_ref[...] = edge
 
 
 def diverge_kernel(
@@ -426,10 +435,9 @@
     return jnp.where((lane == 0) | (lane == nx - 1), moved, 0.0)
 
 
-def first_kernel(zp_ref, px_ref, qa_ref, pb_ref, pz_ref, pd_ref):
+def first_kernel(zp_ref, edge_ref, px_ref, qa_ref, pb_ref, pz_ref, pd_ref):
     fields, ny, nx = zp_ref.shape
     nz = nx // (2 * fields)
-    lane = iota((PTS, nx), 1)
     x_even = lax.axis_index("gx") % 2 == 0
     z_even = lax.axis_index("gz") % 2 == 0
     qa = qa_ref[0:ny]
@@ -441,14 +449,7 @@
     for f in range(fields):
         pz_ref[f * ny : (f + 1) * ny] = zp_ref[f] + place_columns(merged, f * nz, nx)
     pz_ref[fields * ny :] = sums
-    edge = None
-    for e in range(ny // PTS):
-        t = px_ref[e * PTS : (e + 1) * PTS]
-        t = jnp.where(z_even, pltpu.roll(t, nx - 2 * (nz - 1), 1), t)
-        t = pltpu.roll(t, 2 * e, 1) if e else t
-        mine = (lane + 1) % nx // 2 % nz == e
-        edge = jnp.where(mine, t, 0.0 if edge is None else edge)
-    pd_ref[0:PTS] = edge
+    pd_ref[0:PTS] = edge_ref[...]
     pd_ref[PTS:] = sums
 
 
@@ -666,7 +667,11 @@
     table = gll_derivative(ORDER)
     fluxes, px, held, mass, left, right = local_part(table, velocity, geometry, mass_weights)
     qa = lax.ppermute(px, "gx", pairs_near(sizes[0]))
-    zp = call(functools.partial(plane_kernel, table), [(fields, ny, nx)], [fluxes, mass, right])[0]
+    zp, edge = call(
+        functools.partial(plane_kernel, table),
+        [(fields, ny, nx), (PTS, nx)],
+        [fluxes, mass, right, px],
+    )
     pb, pz, pd = call(
         first_kernel,
         [
@@ -674,7 +679,7 @@
             (fields * ny + SCALAR_ROWS, nx),
             (PTS + SCALAR_ROWS, nx),
         ],
-        [zp, px, qa],
+        [zp, edge, px, qa],
     )
     mirror = pairs_mirror(sizes[0])
     qb = lax.ppermute(pb, "gx", mirror)

time: 22.8 us -> 22.7 us (level)
  no operation moved by 1% of the time
where the time goes in v3:
time: 22.7 us; the launch traced here: 22.6 us
  starting transfers between devices  8.91 us (39%)
  Pallas kernels  6.59 us (29%)
  waiting for transfers between devices  6.4 us (28%)
  between operations  0.68 us (3%)
    pallas_call x7, Pallas kernels, call(): pl.pallas_call(kernel, out_shape=[out if hasattr(out, 'dtype') else jax.S...  6.59 us
    ppermute x1, waiting for transfers between devices, few_rounds(): qs = lax.ppermute(ps, ('gx', 'gy'), apart)  3.43 us
    ppermute x1, starting transfers between devices, few_rounds(): qz = lax.ppermute(pz, 'gz', pairs_near(sizes[2]))  2.91 us
    ppermute x1, starting transfers between devices, few_rounds(): qyb = lax.ppermute(pyb, 'gy', pairs_mirror(sizes[1]))  2.47 us
    ppermute x1, waiting for transfers between devices, few_rounds(): qd = lax.ppermute(pd, ('gx', 'gz'), both)  2.36 us
    ppermute x1, starting transfers between devices, few_rounds(): qya = lax.ppermute(pya, 'gy', pairs_near(sizes[1]))  1.64 us
    ppermute x1, starting transfers between devices, few_rounds(): qb = lax.ppermute(pb, 'gx', mirror)  0.98 us
    ppermute x1, waiting for transfers between devices, few_rounds(): qa = lax.ppermute(px, 'gx', pairs_near(sizes[0]))  0.59 us
  transfers between devices with their start and end apart: 7, of which 3 were waited for; matrix products, arithmetic and copies ran while one was open for 0% of the time, Pallas kernels for 9%

profile of v3, /device:TPU:0, one launch (start us, length us, event | category | flops | bytes accessed | tf_op | source)
XLA Modules:
  0.0 22.6 jit_solution(897913283245880826)
XLA Ops:
  0.6 3.1 %shard_map.58 = (f32[3,3,16,32,128]{4,3,2,1,0:T(8,128)S(1)}, f32[40,128]{1,0:T(8,128)S(1)}, f32[3,16,32,128]{3,2,1,0:T(8,128)S(1)}, bf16[16,32,128]{2,1,0:T(8,12...) custom-call(f32[3,16,32,128]{3,2,1,0:T(8,128)} %v_hbm.1, bf16[6,16,32,128]{3,2,1,0:T(8,128)(2,1)} %g_hbm.1, ...), custom_call_target="tpu_custom_call" | custom-call | flops 1048576 | bytes 1048576 | tf_op jit(solution)/shard_map/pallas_call | solution.py:599
  3.7 0.6 %collective-permute-start = (f32[40,128]{1,0:T(8,128)S(1)}, f32[40,128]{1,0:T(8,128)S(1)}, u32[]{:S(2)}, u32[]{:S(2)}) collective-permute-start(f32[40,128]{1,0:T(8,128)S(1)} %get-tuple-element.30.px_ref), channel_id=1, source_target_pairs={{0,8},{8,0},{16,24},{24,16},{1,9},{9,1},{17,25},{25,17},{2,10},{10... | collective-permute-start | bytes 61448 | tf_op jit(solution)/shard_map/ppermute | solution.py:669
  4.3 0.2 %shard_map.60 = (f32[4,32,128]{2,1,0:T(8,128)S(1)}, f32[8,128]{1,0:T(8,128)S(1)}) custom-call(f32[3,3,16,32,128]{4,3,2,1,0:T(8,128)S(1)} %get-tuple-element.25.f_ref, bf16[16,32,128]{2,1,0:T(8,128)(2,1)S(1)} %get-tuple-element.26.m_ref, bf16[4,256,256]{2,1,0:T(8,128)(2,1)S(1)} %get-tuple-element.28.right_ref, f32[40,128]{1,0:T(8,128)S(1)} %get-tuple-element.30.px_ref), custom_call_target="tpu_custom_call" | custom-call | flops 1048576 | bytes 1048576 | tf_op jit(solution)/shard_map/pallas_call | solution.py:599
  4.6 0.6 %collective-permute-done.qa_ref = f32[40,128]{1,0:T(8,128)S(1)} collective-permute-done((f32[40,128]{1,0:T(8,128)S(1)}, f32[40,128]{1,0:T(8,128)S(1)}, u32[]{:S(2)}, u32[]{:S(2)}) %collective-permute-start) | collective-permute-done | bytes 20512 | tf_op jit(solution)/shard_map/ppermute | solution.py:669
  5.1 0.2 shard_map.61
  5.4 2.9 %collective-permute-start.2 = (f32[136,128]{1,0:T(8,128)S(1)}, f32[136,128]{1,0:T(8,128)S(1)}, u32[]{:S(2)}, u32[]{:S(2)}) collective-permute-start(f32[136,128]{1,0:T(8,128)S(1)} %get-tuple-element.34), channel_id=1, source_target_pairs={{0,1},{1,0},{2,3},{3,2},{4,5},{5,4},{6,7},{7,6},{8,9},{9,8},{10,11... | collective-permute-start | bytes 208904 | tf_op jit(solution)/shard_map/ppermute | solution.py:686
  8.3 1.0 %collective-permute-start.1 = (f32[40,128]{1,0:T(8,128)S(1)}, f32[40,128]{1,0:T(8,128)S(1)}, u32[]{:S(2)}, u32[]{:S(2)}) collective-permute-start(f32[40,128]{1,0:T(8,128)S(1)} %get-tuple-element.33.pb_ref), channel_id=1, source_target_pairs={{0,24},{8,16},{16,8},{24,0},{1,25},{9,17},{17,9},{25,1},{2,26},{10... | collective-permute-start | bytes 61448 | tf_op jit(solution)/shard_map/ppermute | solution.py:685
  9.3 0.3 %collective-permute-start.3 = (f32[16,128]{1,0:T(8,128)S(1)}, f32[16,128]{1,0:T(8,128)S(1)}, u32[]{:S(2)}, u32[]{:S(2)}) collective-permute-start(f32[16,128]{1,0:T(8,128)S(1)} %get-tuple-element.35), channel_id=1, source_target_pairs={{0,25},{1,24},{8,17},{9,16},{16,9},{17,8},{24,1},{25,0},{2,27},{3,... | collective-permute-start | bytes 24584 | tf_op jit(solution)/shard_map/ppermute | solution.py:692
  9.5 1.3 %shard_map.59 = (f32[4,16,32,128]{3,2,1,0:T(8,128)S(1)}, f32[2,64,128]{2,1,0:T(8,128)S(1)}) custom-call(f32[3,3,16,32,128]{4,3,2,1,0:T(8,128)S(1)} %get-tuple-element.25.f_ref, bf16[16,32,128]{2,1,0:T(8,128)(2,1)S(1)} %get-tuple-element.26.m_ref, bf16[2,256,768]{2,1,0:T(8,128)(2,1)S(1)} %get-tuple-element.27.left_ref, ...), custom_call_target="tpu_custom_call" | custom-call | flops 1048576 | bytes 1048576 | tf_op jit(solution)/shard_map/pallas_call | solution.py:599
  10.9 2.4 %collective-permute-done.3.qd_ref = f32[16,128]{1,0:T(8,128)S(1)} collective-permute-done((f32[16,128]{1,0:T(8,128)S(1)}, f32[16,128]{1,0:T(8,128)S(1)}, u32[]{:S(2)}, u32[]{:S(2)}) %collective-permute-start.3) | collective-permute-done | bytes 8224 | tf_op jit(solution)/shard_map/ppermute | solution.py:692
  13.2 0.0 collective-permute-done.1.qb_ref
  13.2 0.0 collective-permute-done.2.qz_ref
  13.2 0.2 shard_map.63
  13.4 1.6 %collective-permute-start.4 = (f32[72,128]{1,0:T(8,128)S(1)}, f32[72,128]{1,0:T(8,128)S(1)}, u32[]{:S(2)}, u32[]{:S(2)}) collective-permute-start(f32[72,128]{1,0:T(8,128)S(1)} %get-tuple-element.39), channel_id=1, source_target_pairs={{0,2},{2,0},{4,6},{6,4},{1,3},{3,1},{5,7},{7,5},{8,10},{10,8},{12,... | collective-permute-start | bytes 110600 | tf_op jit(solution)/shard_map/ppermute | solution.py:706
  15.1 2.5 %collective-permute-start.5 = (f32[72,128]{1,0:T(8,128)S(1)}, f32[72,128]{1,0:T(8,128)S(1)}, u32[]{:S(2)}, u32[]{:S(2)}) collective-permute-start(f32[72,128]{1,0:T(8,128)S(1)} %get-tuple-element.40), channel_id=1, source_target_pairs={{0,6},{2,4},{4,2},{6,0},{1,7},{3,5},{5,3},{7,1},{8,14},{10,12},{12... | collective-permute-start | bytes 110600 | tf_op jit(solution)/shard_map/ppermute | solution.py:707
  17.6 0.1 collective-permute-start.6
  17.6 0.4 %shard_map.62 = (f32[4,16,32,128]{3,2,1,0:T(8,128)S(1)}, f32[3,16,32,128]{3,2,1,0:T(8,128)S(1)}) custom-call(f32[3,16,32,128]{3,2,1,0:T(8,128)S(1)} %get-tuple-element.24.v_ref, f32[4,16,32,128]{3,2,1,0:T(8,128)S(1)} %get-tuple-element.29.u_ref, f32[40,128]{1,0:T(8,128)S(1)} %collective-permute-done.qa_ref, f32[40,128]{1,0:T(8,128)S(1)} %collective-permute-done.1.qb_ref, ...), custom_call_target="tpu_custom_call" | custom-call | flops 1048576 | bytes 1048576 | tf_op jit(solution)/shard_map/pallas_call | solution.py:599
  18.1 3.4 %collective-permute-done.6.qs_ref = f32[8,128]{1,0:T(8,128)S(1)} collective-permute-done((f32[8,128]{1,0:T(8,128)S(1)}, f32[8,128]{1,0:T(8,128)S(1)}, u32[]{:S(2)}, u32[]{:S(2)}) %collective-permute-start.6) | collective-permute-done | bytes 4128 | tf_op jit(solution)/shard_map/ppermute | solution.py:708
  21.5 0.0 collective-permute-done.4.qya_ref
  21.5 0.0 collective-permute-done.5.qyb_ref
  21.5 1.1 %shard_map.64 = (f32[3,16,32,128]{3,2,1,0:T(8,128)}, f32[1,1]{1,0:T(1,128)}, f32[1,1]{1,0:T(1,128)}) custom-call(f32[3,16,32,128]{3,2,1,0:T(8,128)S(1)} %get-tuple-element.24.v_ref, f32[4,16,32,128]{3,2,1,0:T(8,128)S(1)} %get-tuple-element.36.w_ref, f32[3,16,32,128]{3,2,1,0:T(8,128)S(1)} %get-tuple-element.37.mv_ref, ...), custom_call_target="tpu_custom_call" | custom-call | flops 1048576 | bytes 1048576 | tf_op jit(solution)/shard_map/pallas_call | solution.py:599
Async XLA Ops:
  3.7 1.4 %collective-permute-start = (f32[40,128]{1,0:T(8,128)S(1)}, f32[40,128]{1,0:T(8,128)S(1)}, u32[]{:S(2)}, u32[]{:S(2)}) collective-permute-start(f32[40,128]{1,0:T(8,128)S(1)} %get-tuple-element.30.px_ref), channel_id=1, source_target_pairs={{0,8},{8,0},{16,24},{24,16},{1,9},{9,1},{17,25},{25,17},{2,10},{10... | collective-permute-start | bytes 61448 | tf_op jit(solution)/shard_map/ppermute | solution.py:669
  5.4 7.9 %collective-permute-start.2 = (f32[136,128]{1,0:T(8,128)S(1)}, f32[136,128]{1,0:T(8,128)S(1)}, u32[]{:S(2)}, u32[]{:S(2)}) collective-permute-start(f32[136,128]{1,0:T(8,128)S(1)} %get-tuple-element.34), channel_id=1, source_target_pairs={{0,1},{1,0},{2,3},{3,2},{4,5},{5,4},{6,7},{7,6},{8,9},{9,8},{10,11... | collective-permute-start | bytes 208904 | tf_op jit(solution)/shard_map/ppermute | solution.py:686
  8.3 5.0 %collective-permute-start.1 = (f32[40,128]{1,0:T(8,128)S(1)}, f32[40,128]{1,0:T(8,128)S(1)}, u32[]{:S(2)}, u32[]{:S(2)}) collective-permute-start(f32[40,128]{1,0:T(8,128)S(1)} %get-tuple-element.33.pb_ref), channel_id=1, source_target_pairs={{0,24},{8,16},{16,8},{24,0},{1,25},{9,17},{17,9},{25,1},{2,26},{10... | collective-permute-start | bytes 61448 | tf_op jit(solution)/shard_map/ppermute | solution.py:685
  9.3 4.0 %collective-permute-start.3 = (f32[16,128]{1,0:T(8,128)S(1)}, f32[16,128]{1,0:T(8,128)S(1)}, u32[]{:S(2)}, u32[]{:S(2)}) collective-permute-start(f32[16,128]{1,0:T(8,128)S(1)} %get-tuple-element.35), channel_id=1, source_target_pairs={{0,25},{1,24},{8,17},{9,16},{16,9},{17,8},{24,1},{25,0},{2,27},{3,... | collective-permute-start | bytes 24584 | tf_op jit(solution)/shard_map/ppermute | solution.py:692
  13.4 8.0 %collective-permute-start.4 = (f32[72,128]{1,0:T(8,128)S(1)}, f32[72,128]{1,0:T(8,128)S(1)}, u32[]{:S(2)}, u32[]{:S(2)}) collective-permute-start(f32[72,128]{1,0:T(8,128)S(1)} %get-tuple-element.39), channel_id=1, source_target_pairs={{0,2},{2,0},{4,6},{6,4},{1,3},{3,1},{5,7},{7,5},{8,10},{10,8},{12,... | collective-permute-start | bytes 110600 | tf_op jit(solution)/shard_map/ppermute | solution.py:706
  15.1 6.4 %collective-permute-start.5 = (f32[72,128]{1,0:T(8,128)S(1)}, f32[72,128]{1,0:T(8,128)S(1)}, u32[]{:S(2)}, u32[]{:S(2)}) collective-permute-start(f32[72,128]{1,0:T(8,128)S(1)} %get-tuple-element.40), channel_id=1, source_target_pairs={{0,6},{2,4},{4,2},{6,0},{1,7},{3,5},{5,3},{7,1},{8,14},{10,12},{12... | collective-permute-start | bytes 110600 | tf_op jit(solution)/shard_map/ppermute | solution.py:707
  17.6 3.9 %collective-permute-start.6 = (f32[8,128]{1,0:T(8,128)S(1)}, f32[8,128]{1,0:T(8,128)S(1)}, u32[]{:S(2)}, u32[]{:S(2)}) collective-permute-start(f32[8,128]{1,0:T(8,128)S(1)} %get-tuple-element.41.ps_ref), channel_id=1, source_target_pairs={{0,12},{2,14},{4,8},{6,10},{8,4},{10,6},{12,0},{14,2},{16,28},{18,... | collective-permute-start | bytes 12296 | tf_op jit(solution)/shard_map/ppermute | solution.py:708

commit v4 on v3

--- a/solution.py
+++ b/solution.py
@@ -537,17 +537,9 @@
     y_even = gy % 2 == 0
     count = fields * nz
     sums = ps_ref[...] + qya_ref[count:] + qyb_ref[count:] + qs_ref[...]
-    kinetic = 0.5 * jnp.sum(sums[0:1])
-    enstrophy = jnp.sum(sums[1:2])
-    kin_ref[0, 0] = kinetic
-    ens_ref[0, 0] = enstrophy
-    copies = [
-        pltpu.make_async_copy(kin_ref, kin_hbm, sems.at[4]),
-        pltpu.make_async_copy(ens_ref, ens_hbm, sems.at[5]),
-    ]
-    for copy in copies:
-        copy.start()
-    rayleigh = jnp.full((PTS, nx), enstrophy, F32) / jnp.full((PTS, nx), 2.0 * kinetic, F32)
+    totals = jnp.sum(sums, axis=1, keepdims=True)
+    kinetic, enstrophy = 0.5 * totals[0:1], totals[1:2]
+    rayleigh = jnp.broadcast_to(enstrophy / (2.0 * kinetic), (PTS, nx))
     low_ref[...] = jnp.where(y_even, qyb_ref[0:count], qya_ref[0:count])
     high_ref[...] = jnp.where(y_even, qya_ref[0:count], qyb_ref[0:count])
     row = iota((ny, nx), 0)
@@ -559,6 +551,7 @@
     inside = (lane != x_first) & (lane != x_last) & (row != y_first) & (row != y_last)
     sub = iota((PTS, nx), 0)
     steps = nz // 4
+    copies = []
     for z in range(nz):
         keep = inside
         if z == 0:
@@ -587,6 +580,15 @@
                 )
             )
             copies[-1].start()
+        if z == steps - 1:
+            kin_ref[0, 0] = kinetic[0, 0]
+            ens_ref[0, 0] = enstrophy[0, 0]
+            for out in (
+                pltpu.make_async_copy(kin_ref, kin_hbm, sems.at[4]),
+                pltpu.make_async_copy(ens_ref, ens_hbm, sems.at[5]),
+            ):
+                out.start()
+                copies.append(out)
     for copy in copies:
         copy.wait()
 

time: 22.7 us -> 22.7 us (level)
  no operation moved by 1% of the time
where the time goes in v4:
time: 22.7 us; the launch traced here: 22.6 us
  starting transfers between devices  8.91 us (39%)
  Pallas kernels  6.59 us (29%)
  waiting for transfers between devices  6.4 us (28%)
  between operations  0.68 us (3%)
    pallas_call x7, Pallas kernels, call(): pl.pallas_call(kernel, out_shape=[out if hasattr(out, 'dtype') else jax.S...  6.59 us
    ppermute x1, waiting for transfers between devices, few_rounds(): qs = lax.ppermute(ps, ('gx', 'gy'), apart)  3.43 us
    ppermute x1, starting transfers between devices, few_rounds(): qz = lax.ppermute(pz, 'gz', pairs_near(sizes[2]))  2.91 us
    ppermute x1, starting transfers between devices, few_rounds(): qyb = lax.ppermute(pyb, 'gy', pairs_mirror(sizes[1]))  2.47 us
    ppermute x1, waiting for transfers between devices, few_rounds(): qd = lax.ppermute(pd, ('gx', 'gz'), both)  2.36 us
    ppermute x1, starting transfers between devices, few_rounds(): qya = lax.ppermute(pya, 'gy', pairs_near(sizes[1]))  1.64 us
    ppermute x1, starting transfers between devices, few_rounds(): qb = lax.ppermute(pb, 'gx', mirror)  0.98 us
    ppermute x1, waiting for transfers between devices, few_rounds(): qa = lax.ppermute(px, 'gx', pairs_near(sizes[0]))  0.59 us
  transfers between devices with their start and end apart: 7, of which 3 were waited for; matrix products, arithmetic and copies ran while one was open for 0% of the time, Pallas kernels for 9%

profile of v4, /device:TPU:0, one launch (start us, length us, event | category | flops | bytes accessed | tf_op | source)
XLA Modules:
  0.0 22.6 jit_solution(4812407275671612541)
XLA Ops:
  0.6 3.1 %shard_map.58 = (f32[3,3,16,32,128]{4,3,2,1,0:T(8,128)S(1)}, f32[40,128]{1,0:T(8,128)S(1)}, f32[3,16,32,128]{3,2,1,0:T(8,128)S(1)}, bf16[16,32,128]{2,1,0:T(8,12...) custom-call(f32[3,16,32,128]{3,2,1,0:T(8,128)} %v_hbm.1, bf16[6,16,32,128]{3,2,1,0:T(8,128)(2,1)} %g_hbm.1, ...), custom_call_target="tpu_custom_call" | custom-call | flops 1048576 | bytes 1048576 | tf_op jit(solution)/shard_map/pallas_call | solution.py:601
  3.7 0.6 %collective-permute-start = (f32[40,128]{1,0:T(8,128)S(1)}, f32[40,128]{1,0:T(8,128)S(1)}, u32[]{:S(2)}, u32[]{:S(2)}) collective-permute-start(f32[40,128]{1,0:T(8,128)S(1)} %get-tuple-element.30.px_ref), channel_id=1, source_target_pairs={{0,8},{8,0},{16,24},{24,16},{1,9},{9,1},{17,25},{25,17},{2,10},{10... | collective-permute-start | bytes 61448 | tf_op jit(solution)/shard_map/ppermute | solution.py:671
  4.3 0.2 %shard_map.60 = (f32[4,32,128]{2,1,0:T(8,128)S(1)}, f32[8,128]{1,0:T(8,128)S(1)}) custom-call(f32[3,3,16,32,128]{4,3,2,1,0:T(8,128)S(1)} %get-tuple-element.25.f_ref, bf16[16,32,128]{2,1,0:T(8,128)(2,1)S(1)} %get-tuple-element.26.m_ref, bf16[4,256,256]{2,1,0:T(8,128)(2,1)S(1)} %get-tuple-element.28.right_ref, f32[40,128]{1,0:T(8,128)S(1)} %get-tuple-element.30.px_ref), custom_call_target="tpu_custom_call" | custom-call | flops 1048576 | bytes 1048576 | tf_op jit(solution)/shard_map/pallas_call | solution.py:601
  4.6 0.6 %collective-permute-done.qa_ref = f32[40,128]{1,0:T(8,128)S(1)} collective-permute-done((f32[40,128]{1,0:T(8,128)S(1)}, f32[40,128]{1,0:T(8,128)S(1)}, u32[]{:S(2)}, u32[]{:S(2)}) %collective-permute-start) | collective-permute-done | bytes 20512 | tf_op jit(solution)/shard_map/ppermute | solution.py:671
  5.1 0.2 shard_map.61
  5.4 2.9 %collective-permute-start.2 = (f32[136,128]{1,0:T(8,128)S(1)}, f32[136,128]{1,0:T(8,128)S(1)}, u32[]{:S(2)}, u32[]{:S(2)}) collective-permute-start(f32[136,128]{1,0:T(8,128)S(1)} %get-tuple-element.34), channel_id=1, source_target_pairs={{0,1},{1,0},{2,3},{3,2},{4,5},{5,4},{6,7},{7,6},{8,9},{9,8},{10,11... | collective-permute-start | bytes 208904 | tf_op jit(solution)/shard_map/ppermute | solution.py:688
  8.3 1.0 %collective-permute-start.1 = (f32[40,128]{1,0:T(8,128)S(1)}, f32[40,128]{1,0:T(8,128)S(1)}, u32[]{:S(2)}, u32[]{:S(2)}) collective-permute-start(f32[40,128]{1,0:T(8,128)S(1)} %get-tuple-element.33.pb_ref), channel_id=1, source_target_pairs={{0,24},{8,16},{16,8},{24,0},{1,25},{9,17},{17,9},{25,1},{2,26},{10... | collective-permute-start | bytes 61448 | tf_op jit(solution)/shard_map/ppermute | solution.py:687
  9.3 0.3 %collective-permute-start.3 = (f32[16,128]{1,0:T(8,128)S(1)}, f32[16,128]{1,0:T(8,128)S(1)}, u32[]{:S(2)}, u32[]{:S(2)}) collective-permute-start(f32[16,128]{1,0:T(8,128)S(1)} %get-tuple-element.35), channel_id=1, source_target_pairs={{0,25},{1,24},{8,17},{9,16},{16,9},{17,8},{24,1},{25,0},{2,27},{3,... | collective-permute-start | bytes 24584 | tf_op jit(solution)/shard_map/ppermute | solution.py:694
  9.5 1.3 %shard_map.59 = (f32[4,16,32,128]{3,2,1,0:T(8,128)S(1)}, f32[2,64,128]{2,1,0:T(8,128)S(1)}) custom-call(f32[3,3,16,32,128]{4,3,2,1,0:T(8,128)S(1)} %get-tuple-element.25.f_ref, bf16[16,32,128]{2,1,0:T(8,128)(2,1)S(1)} %get-tuple-element.26.m_ref, bf16[2,256,768]{2,1,0:T(8,128)(2,1)S(1)} %get-tuple-element.27.left_ref, ...), custom_call_target="tpu_custom_call" | custom-call | flops 1048576 | bytes 1048576 | tf_op jit(solution)/shard_map/pallas_call | solution.py:601
  10.9 2.4 %collective-permute-done.3.qd_ref = f32[16,128]{1,0:T(8,128)S(1)} collective-permute-done((f32[16,128]{1,0:T(8,128)S(1)}, f32[16,128]{1,0:T(8,128)S(1)}, u32[]{:S(2)}, u32[]{:S(2)}) %collective-permute-start.3) | collective-permute-done | bytes 8224 | tf_op jit(solution)/shard_map/ppermute | solution.py:694
  13.2 0.0 collective-permute-done.1.qb_ref
  13.2 0.0 collective-permute-done.2.qz_ref
  13.2 0.2 shard_map.63
  13.4 1.6 %collective-permute-start.4 = (f32[72,128]{1,0:T(8,128)S(1)}, f32[72,128]{1,0:T(8,128)S(1)}, u32[]{:S(2)}, u32[]{:S(2)}) collective-permute-start(f32[72,128]{1,0:T(8,128)S(1)} %get-tuple-element.39), channel_id=1, source_target_pairs={{0,2},{2,0},{4,6},{6,4},{1,3},{3,1},{5,7},{7,5},{8,10},{10,8},{12,... | collective-permute-start | bytes 110600 | tf_op jit(solution)/shard_map/ppermute | solution.py:708
  15.1 2.5 %collective-permute-start.5 = (f32[72,128]{1,0:T(8,128)S(1)}, f32[72,128]{1,0:T(8,128)S(1)}, u32[]{:S(2)}, u32[]{:S(2)}) collective-permute-start(f32[72,128]{1,0:T(8,128)S(1)} %get-tuple-element.40), channel_id=1, source_target_pairs={{0,6},{2,4},{4,2},{6,0},{1,7},{3,5},{5,3},{7,1},{8,14},{10,12},{12... | collective-permute-start | bytes 110600 | tf_op jit(solution)/shard_map/ppermute | solution.py:709
  17.6 0.1 collective-permute-start.6
  17.6 0.4 %shard_map.62 = (f32[4,16,32,128]{3,2,1,0:T(8,128)S(1)}, f32[3,16,32,128]{3,2,1,0:T(8,128)S(1)}) custom-call(f32[3,16,32,128]{3,2,1,0:T(8,128)S(1)} %get-tuple-element.24.v_ref, f32[4,16,32,128]{3,2,1,0:T(8,128)S(1)} %get-tuple-element.29.u_ref, f32[40,128]{1,0:T(8,128)S(1)} %collective-permute-done.qa_ref, f32[40,128]{1,0:T(8,128)S(1)} %collective-permute-done.1.qb_ref, ...), custom_call_target="tpu_custom_call" | custom-call | flops 1048576 | bytes 1048576 | tf_op jit(solution)/shard_map/pallas_call | solution.py:601
  18.1 3.4 %collective-permute-done.6.qs_ref = f32[8,128]{1,0:T(8,128)S(1)} collective-permute-done((f32[8,128]{1,0:T(8,128)S(1)}, f32[8,128]{1,0:T(8,128)S(1)}, u32[]{:S(2)}, u32[]{:S(2)}) %collective-permute-start.6) | collective-permute-done | bytes 4128 | tf_op jit(solution)/shard_map/ppermute | solution.py:710
  21.5 0.0 collective-permute-done.4.qya_ref
  21.5 0.0 collective-permute-done.5.qyb_ref
  21.5 1.1 %shard_map.64 = (f32[3,16,32,128]{3,2,1,0:T(8,128)}, f32[1,1]{1,0:T(1,128)}, f32[1,1]{1,0:T(1,128)}) custom-call(f32[3,16,32,128]{3,2,1,0:T(8,128)S(1)} %get-tuple-element.24.v_ref, f32[4,16,32,128]{3,2,1,0:T(8,128)S(1)} %get-tuple-element.36.w_ref, f32[3,16,32,128]{3,2,1,0:T(8,128)S(1)} %get-tuple-element.37.mv_ref, ...), custom_call_target="tpu_custom_call" | custom-call | flops 1048576 | bytes 1048576 | tf_op jit(solution)/shard_map/pallas_call | solution.py:601
Async XLA Ops:
  3.7 1.4 %collective-permute-start = (f32[40,128]{1,0:T(8,128)S(1)}, f32[40,128]{1,0:T(8,128)S(1)}, u32[]{:S(2)}, u32[]{:S(2)}) collective-permute-start(f32[40,128]{1,0:T(8,128)S(1)} %get-tuple-element.30.px_ref), channel_id=1, source_target_pairs={{0,8},{8,0},{16,24},{24,16},{1,9},{9,1},{17,25},{25,17},{2,10},{10... | collective-permute-start | bytes 61448 | tf_op jit(solution)/shard_map/ppermute | solution.py:671
  5.4 7.9 %collective-permute-start.2 = (f32[136,128]{1,0:T(8,128)S(1)}, f32[136,128]{1,0:T(8,128)S(1)}, u32[]{:S(2)}, u32[]{:S(2)}) collective-permute-start(f32[136,128]{1,0:T(8,128)S(1)} %get-tuple-element.34), channel_id=1, source_target_pairs={{0,1},{1,0},{2,3},{3,2},{4,5},{5,4},{6,7},{7,6},{8,9},{9,8},{10,11... | collective-permute-start | bytes 208904 | tf_op jit(solution)/shard_map/ppermute | solution.py:688
  8.3 5.0 %collective-permute-start.1 = (f32[40,128]{1,0:T(8,128)S(1)}, f32[40,128]{1,0:T(8,128)S(1)}, u32[]{:S(2)}, u32[]{:S(2)}) collective-permute-start(f32[40,128]{1,0:T(8,128)S(1)} %get-tuple-element.33.pb_ref), channel_id=1, source_target_pairs={{0,24},{8,16},{16,8},{24,0},{1,25},{9,17},{17,9},{25,1},{2,26},{10... | collective-permute-start | bytes 61448 | tf_op jit(solution)/shard_map/ppermute | solution.py:687
  9.3 4.0 %collective-permute-start.3 = (f32[16,128]{1,0:T(8,128)S(1)}, f32[16,128]{1,0:T(8,128)S(1)}, u32[]{:S(2)}, u32[]{:S(2)}) collective-permute-start(f32[16,128]{1,0:T(8,128)S(1)} %get-tuple-element.35), channel_id=1, source_target_pairs={{0,25},{1,24},{8,17},{9,16},{16,9},{17,8},{24,1},{25,0},{2,27},{3,... | collective-permute-start | bytes 24584 | tf_op jit(solution)/shard_map/ppermute | solution.py:694
  13.4 8.0 %collective-permute-start.4 = (f32[72,128]{1,0:T(8,128)S(1)}, f32[72,128]{1,0:T(8,128)S(1)}, u32[]{:S(2)}, u32[]{:S(2)}) collective-permute-start(f32[72,128]{1,0:T(8,128)S(1)} %get-tuple-element.39), channel_id=1, source_target_pairs={{0,2},{2,0},{4,6},{6,4},{1,3},{3,1},{5,7},{7,5},{8,10},{10,8},{12,... | collective-permute-start | bytes 110600 | tf_op jit(solution)/shard_map/ppermute | solution.py:708
  15.1 6.4 %collective-permute-start.5 = (f32[72,128]{1,0:T(8,128)S(1)}, f32[72,128]{1,0:T(8,128)S(1)}, u32[]{:S(2)}, u32[]{:S(2)}) collective-permute-start(f32[72,128]{1,0:T(8,128)S(1)} %get-tuple-element.40), channel_id=1, source_target_pairs={{0,6},{2,4},{4,2},{6,0},{1,7},{3,5},{5,3},{7,1},{8,14},{10,12},{12... | collective-permute-start | bytes 110600 | tf_op jit(solution)/shard_map/ppermute | solution.py:709
  17.6 3.9 %collective-permute-start.6 = (f32[8,128]{1,0:T(8,128)S(1)}, f32[8,128]{1,0:T(8,128)S(1)}, u32[]{:S(2)}, u32[]{:S(2)}) collective-permute-start(f32[8,128]{1,0:T(8,128)S(1)} %get-tuple-element.41.ps_ref), channel_id=1, source_target_pairs={{0,12},{2,14},{4,8},{6,10},{8,4},{10,6},{12,0},{14,2},{16,28},{18,... | collective-permute-start | bytes 12296 | tf_op jit(solution)/shard_map/ppermute | solution.py:710
